TPU v7x, 16 devices: a 4x2x1 block of a 4x4x8 slice. The times are simulated.
16 devices in a mesh: dp: 2 (over y, z), tp: 8 (over x, core).
Axes of the slice: x: 4, y: 2, z: 1, core: 2. Of those that a mesh axis runs over, the one named last changes fastest.
The devices are a block of a 4x4x8 slice.
Arguments:
- x_in: bfloat16 [2, 2048, 1024], P(None, ('dp', 'tp')), parts along dimension 1
- y_cot: bfloat16 [2, 2048, 1024], P(None, ('dp', 'tp')), parts along dimension 1
- gain_attn: float32 [2, 1024], replicated
- gain_mlp: float32 [2, 1024], replicated
- w_qkv: bfloat16 [2, 1024, 8, 4, 128], P(None, None, 'tp')
- w_out: bfloat16 [2, 16, 128, 1024], P(None, 'tp')
- w_gate: bfloat16 [2, 1024, 3072], P(None, None, 'tp')
- w_up: bfloat16 [2, 1024, 3072], P(None, None, 'tp')
- w_down: bfloat16 [2, 3072, 1024], P(None, 'tp')
Outputs:
- output 1: bfloat16 [2, 2048, 1024], P(None, ('dp', 'tp')), parts along dimension 1
- output 2: bfloat16 [2, 2048, 1024], P(None, ('dp', 'tp')), parts along dimension 1
- output 3: bfloat16 [4, 1024, 8, 4, 128], P('dp', None, 'tp'), parts along dimension 0
- output 4: bfloat16 [4, 16, 128, 1024], P('dp', 'tp'), parts along dimension 0
- output 5: bfloat16 [4, 1024, 3072], P('dp', None, 'tp'), parts along dimension 0
- output 6: bfloat16 [4, 1024, 3072], P('dp', None, 'tp'), parts along dimension 0
- output 7: bfloat16 [4, 3072, 1024], P('dp', 'tp'), parts along dimension 0
- output 8: float32 [4, 1024], P('dp'), parts along dimension 0
- output 9: float32 [4, 1024], P('dp'), parts along dimension 0
There are 2 independent parts. A program takes and returns all parts, laid end to end along the dimension named above; an argument that names none is the same for every part.
All inputs are finite; a program needn't handle non-finite values.
Results may differ from a plain program's by a relative error of at most 0.02.
Values are sent between devices in bfloat16 or wider.
A program may use at most 768 MiB of HBM per device.

v0:
```python
import jax
import jax.numpy as jnp
from jax import lax
from jax.sharding import PartitionSpec as P

NORM_EPS = 1e-5


def rms_scale(row_vals, gain_vec):
    return row_vals * lax.rsqrt(jnp.mean(row_vals * row_vals, axis=-1, keepdims=True) + NORM_EPS) * gain_vec


def norm_apply(row_vals, gain_vec):
    return rms_scale(row_vals.astype(jnp.float32), gain_vec).astype(jnp.bfloat16)


def norm_backward(row_vals, gain_vec, cot_rows):
    unused, pull = jax.vjp(rms_scale, row_vals.astype(jnp.float32), gain_vec)
    return pull(cot_rows.astype(jnp.float32))


def causal_mask(seq_len):
    row_pos = lax.broadcasted_iota(jnp.int32, (seq_len, 1, seq_len), 0)
    col_pos = lax.broadcasted_iota(jnp.int32, (seq_len, 1, seq_len), 2)
    return row_pos >= col_pos


def attention_forward(queries, key_heads, value_heads, score_scale):
    seq_len = queries.shape[0]
    scores = jnp.einsum('qkge,tke->kqgt', queries, key_heads, preferred_element_type=jnp.float32) * score_scale
    scores = jnp.where(causal_mask(seq_len), scores, -1e30)
    row_max = jnp.max(scores, axis=-1, keepdims=True)
    exp_scores = jnp.exp(scores - row_max)
    row_total = jnp.sum(exp_scores, axis=-1, keepdims=True)
    prob_b16 = (exp_scores / row_total).astype(jnp.bfloat16)
    attn_mix = jnp.einsum('kqgt,tke->kqge', prob_b16, value_heads, preferred_element_type=jnp.float32).astype(jnp.bfloat16)
    return attn_mix, row_max + jnp.log(row_total)


def attention_backward(queries, key_heads, value_heads, log_norm, grad_mix, score_scale):
    seq_len = queries.shape[0]
    scores = jnp.einsum('qkge,tke->kqgt', queries, key_heads, preferred_element_type=jnp.float32) * score_scale
    scores = jnp.where(causal_mask(seq_len), scores, -1e30)
    prob_f32 = jnp.exp(scores - log_norm)
    prob_b16 = prob_f32.astype(jnp.bfloat16)
    grad_prob = jnp.einsum('qkge,tke->kqgt', grad_mix, value_heads, preferred_element_type=jnp.float32).astype(jnp.bfloat16).astype(jnp.float32)
    row_dot = jnp.sum(grad_prob * prob_f32, axis=-1, keepdims=True)
    grad_scores = (prob_f32 * (grad_prob - row_dot) * score_scale).astype(jnp.bfloat16)
    grad_q = jnp.einsum('kqgt,tke->qkge', grad_scores, key_heads, preferred_element_type=jnp.float32)
    grad_k = jnp.einsum('kqgt,qkge->tke', grad_scores, queries, preferred_element_type=jnp.float32)
    grad_v = jnp.einsum('kqgt,qkge->tke', prob_b16, grad_mix, preferred_element_type=jnp.float32)
    return grad_q, grad_k, grad_v


def solution(mesh):
    row_spec = P(None, ('dp', 'tp'), None)
    gain_spec = P(None, None)
    qkv_spec = P(None, None, 'tp', None, None)
    head_spec = P(None, 'tp', None, None)
    col_spec = P(None, None, 'tp')
    row_shard_spec = P(None, 'tp', None)

    def device_program(x_in, y_cot, gain_attn, gain_mlp, w_qkv, w_out, w_gate, w_up, w_down):
        micro_count = x_in.shape[0]
        width = x_in.shape[2]
        layer_count = w_qkv.shape[0]
        kv_local = w_qkv.shape[2]
        groups = w_qkv.shape[3] - 2
        head_dim = w_qkv.shape[4]
        score_scale = head_dim ** -0.5
        kept_acts = []
        y_rows = []
        for micro_idx in range(micro_count):
            layer_in = x_in[micro_idx]
            per_layer = []
            for layer_idx in range(layer_count):
                normed = norm_apply(layer_in, gain_attn[layer_idx])
                normed_full = lax.all_gather(normed, 'tp', axis=0, tiled=True)
                qkv_heads = jnp.einsum('sd,dkje->skje', normed_full, w_qkv[layer_idx], preferred_element_type=jnp.float32).astype(jnp.bfloat16)
                queries = qkv_heads[:, :, :groups]
                key_heads = qkv_heads[:, :, groups]
                value_heads = qkv_heads[:, :, groups + 1]
                attn_mix, log_norm = attention_forward(queries, key_heads, value_heads, score_scale)
                heads_out = w_out[layer_idx].reshape(kv_local, groups, head_dim, width)
                attn_part = jnp.einsum('kqge,kged->qd', attn_mix, heads_out, preferred_element_type=jnp.float32)
                attn_sum = lax.psum_scatter(attn_part, 'tp', scatter_dimension=0, tiled=True).astype(jnp.bfloat16)
                hidden = (layer_in.astype(jnp.float32) + attn_sum.astype(jnp.float32)).astype(jnp.bfloat16)
                normed_b = norm_apply(hidden, gain_mlp[layer_idx])
                normed_b_full = lax.all_gather(normed_b, 'tp', axis=0, tiled=True)
                gate_pre = jnp.dot(normed_b_full, w_gate[layer_idx], preferred_element_type=jnp.float32)
                up_proj = jnp.dot(normed_b_full, w_up[layer_idx], preferred_element_type=jnp.float32)
                inner = (jax.nn.silu(gate_pre) * up_proj).astype(jnp.bfloat16)
                down_part = jnp.dot(inner, w_down[layer_idx], preferred_element_type=jnp.float32)
                mlp_sum = lax.psum_scatter(down_part, 'tp', scatter_dimension=0, tiled=True).astype(jnp.bfloat16)
                per_layer.append((layer_in, normed, hidden, normed_b, queries, key_heads, value_heads, attn_mix, log_norm))
                layer_in = (hidden.astype(jnp.float32) + mlp_sum.astype(jnp.float32)).astype(jnp.bfloat16)
            kept_acts.append(per_layer)
            y_rows.append(layer_in)

        grad_qkv_acc = [None] * layer_count
        grad_out_acc = [None] * layer_count
        grad_gate_acc = [None] * layer_count
        grad_up_acc = [None] * layer_count
        grad_down_acc = [None] * layer_count
        gain_a_acc = [None] * layer_count
        gain_b_acc = [None] * layer_count

        def accumulate(acc_list, layer_idx, term):
            acc_list[layer_idx] = term if acc_list[layer_idx] is None else acc_list[layer_idx] + term

        grad_rows = []
        for micro_idx in range(micro_count):
            grad_in = y_cot[micro_idx]
            for layer_idx in reversed(range(layer_count)):
                layer_in, normed, hidden, normed_b, queries, key_heads, value_heads, attn_mix, log_norm = kept_acts[micro_idx][layer_idx]
                normed_b_full = lax.all_gather(normed_b, 'tp', axis=0, tiled=True)
                grad_full = lax.all_gather(grad_in, 'tp', axis=0, tiled=True)
                gate_pre = jnp.dot(normed_b_full, w_gate[layer_idx], preferred_element_type=jnp.float32)
                up_proj = jnp.dot(normed_b_full, w_up[layer_idx], preferred_element_type=jnp.float32)
                gate_sig = jax.nn.sigmoid(gate_pre)
                gate_act = gate_pre * gate_sig
                inner = (gate_act * up_proj).astype(jnp.bfloat16)
                accumulate(grad_down_acc, layer_idx, jnp.einsum('sf,sd->fd', inner, grad_full, preferred_element_type=jnp.float32))
                grad_inner = jnp.einsum('sd,fd->sf', grad_full, w_down[layer_idx], preferred_element_type=jnp.float32).astype(jnp.bfloat16).astype(jnp.float32)
                grad_up = (grad_inner * gate_act).astype(jnp.bfloat16)
                grad_gate = (grad_inner * up_proj * gate_sig * (1.0 + gate_pre * (1.0 - gate_sig))).astype(jnp.bfloat16)
                accumulate(grad_gate_acc, layer_idx, jnp.einsum('sd,sf->df', normed_b_full, grad_gate, preferred_element_type=jnp.float32))
                accumulate(grad_up_acc, layer_idx, jnp.einsum('sd,sf->df', normed_b_full, grad_up, preferred_element_type=jnp.float32))
                grad_nb_part = jnp.einsum('sf,df->sd', grad_gate, w_gate[layer_idx], preferred_element_type=jnp.float32) + jnp.einsum('sf,df->sd', grad_up, w_up[layer_idx], preferred_element_type=jnp.float32)
                grad_nb = lax.psum_scatter(grad_nb_part, 'tp', scatter_dimension=0, tiled=True).astype(jnp.bfloat16)
                grad_h_norm, grad_gain_b = norm_backward(hidden, gain_mlp[layer_idx], grad_nb)
                accumulate(gain_b_acc, layer_idx, grad_gain_b)
                grad_hidden = (grad_in.astype(jnp.float32) + grad_h_norm).astype(jnp.bfloat16)
                normed_full = lax.all_gather(normed, 'tp', axis=0, tiled=True)
                grad_hfull = lax.all_gather(grad_hidden, 'tp', axis=0, tiled=True)
                heads_out = w_out[layer_idx].reshape(kv_local, groups, head_dim, width)
                accumulate(grad_out_acc, layer_idx, jnp.einsum('kqge,qd->kged', attn_mix, grad_hfull, preferred_element_type=jnp.float32).reshape(w_out.shape[1:]))
                grad_mix = jnp.einsum('qd,kged->qkge', grad_hfull, heads_out, preferred_element_type=jnp.float32).astype(jnp.bfloat16)
                grad_q, grad_k, grad_v = attention_backward(queries, key_heads, value_heads, log_norm, grad_mix, score_scale)
                grad_qkv = jnp.concatenate([grad_q, grad_k[:, :, None], grad_v[:, :, None]], axis=2).astype(jnp.bfloat16)
                accumulate(grad_qkv_acc, layer_idx, jnp.einsum('sd,skje->dkje', normed_full, grad_qkv, preferred_element_type=jnp.float32))
                grad_n_part = jnp.einsum('skje,dkje->sd', grad_qkv, w_qkv[layer_idx], preferred_element_type=jnp.float32)
                grad_n = lax.psum_scatter(grad_n_part, 'tp', scatter_dimension=0, tiled=True).astype(jnp.bfloat16)
                grad_x_norm, grad_gain_a = norm_backward(layer_in, gain_attn[layer_idx], grad_n)
                accumulate(gain_a_acc, layer_idx, grad_gain_a)
                grad_in = (grad_hidden.astype(jnp.float32) + grad_x_norm).astype(jnp.bfloat16)
            grad_rows.append(grad_in)

        gain_grads = lax.psum(jnp.stack([jnp.stack(gain_a_acc), jnp.stack(gain_b_acc)]), 'tp')
        return (jnp.stack(y_rows), jnp.stack(grad_rows),
                jnp.stack([item.astype(jnp.bfloat16) for item in grad_qkv_acc]),
                jnp.stack([item.astype(jnp.bfloat16) for item in grad_out_acc]),
                jnp.stack([item.astype(jnp.bfloat16) for item in grad_gate_acc]),
                jnp.stack([item.astype(jnp.bfloat16) for item in grad_up_acc]),
                jnp.stack([item.astype(jnp.bfloat16) for item in grad_down_acc]),
                gain_grads[0], gain_grads[1])

    return jax.shard_map(device_program, mesh=mesh,
                         in_specs=(row_spec, row_spec, gain_spec, gain_spec, qkv_spec, head_spec, col_spec, col_spec, row_shard_spec),
                         out_specs=(row_spec, row_spec, P('dp', None, 'tp', None, None), P('dp', 'tp', None, None), P('dp', None, 'tp'), P('dp', None, 'tp'), P('dp', 'tp', None), P('dp', None), P('dp', None)),
                         check_vma=False)
```

profile of v0, /device:TPU:113, one launch (start us, length us, event | category | flops | bytes accessed | tf_op | source)
XLA Modules:
  0.0 1069.7 jit_solution(10390321871312252858)
XLA Ops:
  15.9 21.1 %all-gather.19.cloned.1.call-done = bf16[1024,1024]{1,0:T(8,128)(2,1)} async-done(((bf16[128,1024]{1,0:T(8,128)(2,1)}), bf16[1024,1024]{1,0:T(8,128)(2,1)}) %all-gather.19.cloned.1.call-update) | async-done | bytes 2097168 | tf_op jit(solution)/shard_map/all_gather | solution.py:78
  51.0 9.8 all-gather.27.cloned.1.call-done
  74.9 19.4 %reduce-scatter.17.cloned.1.call-done = f32[128,1024]{1,0:T(8,128)} async-done(((f32[1024,1024]{1,0:T(8,128)}), f32[128,1024]{1,0:T(8,128)}) %reduce-scatter.17.cloned.1.call-update) | async-done | bytes 524304 | tf_op jit(solution)/shard_map/reduce_scatter | solution.py:86
  94.3 34.9 %reduce-scatter.25.cloned.1.call-done = f32[128,1024]{1,0:T(8,128)} async-done(((f32[1024,1024]{1,0:T(8,128)}), f32[128,1024]{1,0:T(8,128)}) %reduce-scatter.25.cloned.1.call-update) | async-done | bytes 524304 | tf_op jit(solution)/shard_map/reduce_scatter | solution.py:86
  133.0 22.6 %all-gather.29.cloned.1.call-done = bf16[1024,1024]{1,0:T(8,128)(2,1)} async-done(((bf16[128,1024]{1,0:T(8,128)(2,1)}), bf16[1024,1024]{1,0:T(8,128)(2,1)}) %all-gather.29.cloned.1.call-update) | async-done | bytes 2097168 | tf_op jit(solution)/shard_map/all_gather | solution.py:89
  162.0 3.3 fusion.278
  165.8 13.4 %all-gather.21.cloned.1.call-done = bf16[1024,1024]{1,0:T(8,128)(2,1)} async-done(((bf16[128,1024]{1,0:T(8,128)(2,1)}), bf16[1024,1024]{1,0:T(8,128)(2,1)}) %all-gather.21.cloned.1.call-update) | async-done | bytes 2097168 | tf_op jit(solution)/shard_map/all_gather | solution.py:89
  179.2 3.2 fusion.294
  185.7 3.3 fusion.280
  189.1 23.6 %reduce-scatter.27.cloned.1.call-done = f32[128,1024]{1,0:T(8,128)} async-done(((f32[1024,1024]{1,0:T(8,128)}), f32[128,1024]{1,0:T(8,128)}) %reduce-scatter.27.cloned.1.call-update) | async-done | bytes 524304 | tf_op jit(solution)/shard_map/reduce_scatter | solution.py:94
  213.9 33.8 %reduce-scatter.19.cloned.1.call-done = f32[128,1024]{1,0:T(8,128)} async-done(((f32[1024,1024]{1,0:T(8,128)}), f32[128,1024]{1,0:T(8,128)}) %reduce-scatter.19.cloned.1.call-update) | async-done | bytes 524304 | tf_op jit(solution)/shard_map/reduce_scatter | solution.py:94
  250.0 23.1 %all-gather.23.cloned.1.call-done = bf16[1024,1024]{1,0:T(8,128)(2,1)} async-done(((bf16[128,1024]{1,0:T(8,128)(2,1)}), bf16[1024,1024]{1,0:T(8,128)(2,1)}) %all-gather.23.cloned.1.call-update) | async-done | bytes 2097168 | tf_op jit(solution)/shard_map/all_gather | solution.py:78
  273.2 3.2 fusion.146
  289.0 29.4 %reduce-scatter.21.cloned.1.call-done = f32[128,1024]{1,0:T(8,128)} async-done(((f32[1024,1024]{1,0:T(8,128)}), f32[128,1024]{1,0:T(8,128)}) %reduce-scatter.21.cloned.1.call-update) | async-done | bytes 524304 | tf_op jit(solution)/shard_map/reduce_scatter | solution.py:86
  321.5 22.3 %all-gather.31.cloned.1.call-done = bf16[1024,1024]{1,0:T(8,128)(2,1)} async-done(((bf16[128,1024]{1,0:T(8,128)(2,1)}), bf16[1024,1024]{1,0:T(8,128)(2,1)}) %all-gather.31.cloned.1.call-update) | async-done | bytes 2097168 | tf_op jit(solution)/shard_map/all_gather | solution.py:78
  343.8 3.2 fusion.140
  357.5 9.4 all-gather.47.cloned.1.call-done
  366.9 3.8 fusion.134
  370.6 19.5 %all-gather.25.cloned.1.call-done = bf16[1024,1024]{1,0:T(8,128)(2,1)} async-done(((bf16[128,1024]{1,0:T(8,128)(2,1)}), bf16[1024,1024]{1,0:T(8,128)(2,1)}) %all-gather.25.cloned.1.call-update) | async-done | bytes 2097168 | tf_op jit(solution)/shard_map/all_gather | solution.py:89
  396.5 3.2 convolution_add_fusion.3
  400.7 22.8 %reduce-scatter.29.cloned.1.call-done = f32[128,1024]{1,0:T(8,128)} async-done(((f32[1024,1024]{1,0:T(8,128)}), f32[128,1024]{1,0:T(8,128)}) %reduce-scatter.29.cloned.1.call-update) | async-done | bytes 524304 | tf_op jit(solution)/shard_map/reduce_scatter | solution.py:86
  425.3 33.1 %reduce-scatter.33.cloned.1.call-done = f32[128,1024]{1,0:T(8,128)} async-done(((f32[1024,1024]{1,0:T(8,128)}), f32[128,1024]{1,0:T(8,128)}) %reduce-scatter.33.cloned.1.call-update) | async-done | bytes 524304 | tf_op jit(solution)/shard_map/reduce_scatter | solution.py:130
  460.7 22.3 %all-gather.49.cloned.1.call-done = bf16[1,1024,1024]{2,1,0:T(8,128)(2,1)} async-done(((bf16[1,128,1024]{2,1,0:T(8,128)(2,1)}), bf16[1,1024,1024]{2,1,0:T(8,128)(2,1)}) %all-gather.49.cloned.1.call-update) | async-done | bytes 2097168 | tf_op jit(solution)/shard_map/all_gather | solution.py:117
  483.0 3.8 fusion.137
  486.8 19.3 %all-gather.33.cloned.1.call-done = bf16[1024,1024]{1,0:T(8,128)(2,1)} async-done(((bf16[128,1024]{1,0:T(8,128)(2,1)}), bf16[1024,1024]{1,0:T(8,128)(2,1)}) %all-gather.33.cloned.1.call-update) | async-done | bytes 2097168 | tf_op jit(solution)/shard_map/all_gather | solution.py:89
  506.1 3.2 fusion.272
  514.2 3.3 convolution_add_fusion.1
  517.6 3.2 fusion.260
  520.9 4.5 fusion.258
  525.6 23.2 %reduce-scatter.41.cloned.1.call-done = f32[128,1024]{1,0:T(8,128)} async-done(((f32[1024,1024]{1,0:T(8,128)}), f32[128,1024]{1,0:T(8,128)}) %reduce-scatter.41.cloned.1.call-update) | async-done | bytes 524304 | tf_op jit(solution)/shard_map/reduce_scatter | solution.py:130
  550.1 33.8 %reduce-scatter.23.cloned.1.call-done = f32[128,1024]{1,0:T(8,128)} async-done(((f32[1024,1024]{1,0:T(8,128)}), f32[128,1024]{1,0:T(8,128)}) %reduce-scatter.23.cloned.1.call-update) | async-done | bytes 524304 | tf_op jit(solution)/shard_map/reduce_scatter | solution.py:94
  583.9 34.9 %reduce-scatter.31.cloned.1.call-done = f32[128,1024]{1,0:T(8,128)} async-done(((f32[1024,1024]{1,0:T(8,128)}), f32[128,1024]{1,0:T(8,128)}) %reduce-scatter.31.cloned.1.call-update) | async-done | bytes 524304 | tf_op jit(solution)/shard_map/reduce_scatter | solution.py:94
  623.3 22.0 %all-gather.41.cloned.1.call-done = bf16[1024,1024]{1,0:T(8,128)(2,1)} async-done(((bf16[128,1024]{1,0:T(8,128)(2,1)}), bf16[1024,1024]{1,0:T(8,128)(2,1)}) %all-gather.41.cloned.1.call-update) | async-done | bytes 2097168 | tf_op jit(solution)/shard_map/all_gather | solution.py:135
  648.5 4.2 convolution_convert_fusion.1
  652.7 13.3 %fusion.254 = bf16[1024,1,128]{0,2,1:T(8,128)(2,1)} fusion(bf16[1024,2,1024]{0,2,1:T(8,128)(2,1)} %convolution_convert_fusion.1, f32[1024,2,1024]{0,2,1:T(8,128)} %copy-done.3, f32[1024,2]{0,1:T(2,128)S(1)} %log_add_fusion.1, bf16[1024,1,4,128]{3,0,2,1:T(8,128)(2,1)} %copy-done.97), kind=kOutput, calls=%fused_computation.245 | convolution fusion | flops 555879424 | bytes 25968640 | tf_op jit(solution)/shard_map/kqgt,qkge->tke/dot_general | solution.py:50
  666.0 13.3 %fusion.205 = bf16[1024,2,128]{0,2,1:T(8,128)(2,1)} fusion(bf16[1024,2,1024]{0,2,1:T(8,128)(2,1)} %convolution_convert_fusion.1, f32[1024,2,1024]{0,2,1:T(8,128)} %copy-done.3, f32[1024,2]{0,1:T(2,128)S(1)} %log_add_fusion.1, bf16[1024,1,4,128]{3,0,2,1:T(8,128)(2,1)} %copy-done.97), kind=kOutput, calls=%fused_computation.220 | convolution fusion | flops 556010496 | bytes 25968640 | tf_op jit(solution)/shard_map/kqgt,tke->qkge/dot_general | solution.py:49
  679.3 5.2 fusion.246
  685.3 3.6 convolution_bitcast_fusion.1
  692.3 4.1 convolution_convert_fusion.3
  696.4 13.7 %fusion.252 = bf16[1024,1,128]{0,2,1:T(8,128)(2,1)} fusion(bf16[1024,2,1024]{0,2,1:T(8,128)(2,1)} %convolution_convert_fusion.3, f32[1024,2,1024]{0,2,1:T(8,128)} %copy-done.2, f32[1024,2]{0,1:T(2,128)S(1)} %log_add_fusion.3, bf16[1024,1,4,128]{3,0,2,1:T(8,128)(2,1)} %copy-done.96), kind=kOutput, calls=%fused_computation.243 | convolution fusion | flops 555879424 | bytes 25968640 | tf_op jit(solution)/shard_map/kqgt,qkge->tke/dot_general | solution.py:50
  710.1 13.8 %fusion.207 = bf16[1024,2,128]{0,2,1:T(8,128)(2,1)} fusion(bf16[1024,2,1024]{0,2,1:T(8,128)(2,1)} %convolution_convert_fusion.3, f32[1024,2,1024]{0,2,1:T(8,128)} %copy-done.2, f32[1024,2]{0,1:T(2,128)S(1)} %log_add_fusion.3, bf16[1024,1,4,128]{3,0,2,1:T(8,128)(2,1)} %copy-done.96), kind=kOutput, calls=%fused_computation.222 | convolution fusion | flops 556010496 | bytes 25968640 | tf_op jit(solution)/shard_map/kqgt,tke->qkge/dot_general | solution.py:49
  723.9 5.2 fusion.240
  729.9 3.6 convolution_bitcast_fusion.3
  733.6 31.2 %reduce-scatter.35.cloned.1.call-done = f32[128,1024]{1,0:T(8,128)} async-done(((f32[1024,1024]{1,0:T(8,128)}), f32[128,1024]{1,0:T(8,128)}) %reduce-scatter.35.cloned.1.call-update) | async-done | bytes 524304 | tf_op jit(solution)/shard_map/reduce_scatter | solution.py:143
  769.6 22.6 %all-gather.43.cloned.1.call-done = bf16[1024,1024]{1,0:T(8,128)(2,1)} async-done(((bf16[128,1024]{1,0:T(8,128)(2,1)}), bf16[1024,1024]{1,0:T(8,128)(2,1)}) %all-gather.43.cloned.1.call-update) | async-done | bytes 2097168 | tf_op jit(solution)/shard_map/all_gather | solution.py:117
  792.3 4.2 fusion.110
  798.9 3.3 convolution_add_fusion
  802.4 13.5 %all-gather.37.cloned.1.call-done = bf16[1024,1024]{1,0:T(8,128)(2,1)} async-done(((bf16[128,1024]{1,0:T(8,128)(2,1)}), bf16[1024,1024]{1,0:T(8,128)(2,1)}) %all-gather.37.cloned.1.call-update) | async-done | bytes 2097168 | tf_op jit(solution)/shard_map/all_gather | solution.py:117
  815.9 4.4 fusion.103
  822.3 3.3 convolution_add_fusion.2
  825.8 23.5 %reduce-scatter.45.cloned.1.call-done = f32[128,1024]{1,0:T(8,128)} async-done(((f32[1024,1024]{1,0:T(8,128)}), f32[128,1024]{1,0:T(8,128)}) %reduce-scatter.45.cloned.1.call-update) | async-done | bytes 524304 | tf_op jit(solution)/shard_map/reduce_scatter | solution.py:130
  849.3 35.1 %reduce-scatter.37.cloned.1.call-done = f32[128,1024]{1,0:T(8,128)} async-done(((f32[1024,1024]{1,0:T(8,128)}), f32[128,1024]{1,0:T(8,128)}) %reduce-scatter.37.cloned.1.call-update) | async-done | bytes 524304 | tf_op jit(solution)/shard_map/reduce_scatter | solution.py:130
  889.6 22.0 %all-gather.45.cloned.1.call-done = bf16[1024,1024]{1,0:T(8,128)(2,1)} async-done(((bf16[128,1024]{1,0:T(8,128)(2,1)}), bf16[1024,1024]{1,0:T(8,128)(2,1)}) %all-gather.45.cloned.1.call-update) | async-done | bytes 2097168 | tf_op jit(solution)/shard_map/all_gather | solution.py:135
  914.0 4.2 convolution_convert_fusion
  918.2 13.3 %fusion.255 = bf16[1024,1,128]{0,2,1:T(8,128)(2,1)} fusion(bf16[1024,2,1024]{0,2,1:T(8,128)(2,1)} %convolution_convert_fusion, f32[1024,2,1024]{0,2,1:T(8,128)} %copy-done.1, f32[1024,2]{0,1:T(2,128)S(1)} %log_add_fusion, bf16[1024,1,4,128]{3,0,2,1:T(8,128)(2,1)} %copy-done.95), kind=kOutput, calls=%fused_computation.246 | convolution fusion | flops 555879424 | bytes 25968640 | tf_op jit(solution)/shard_map/kqgt,qkge->tke/dot_general | solution.py:50
  931.6 12.5 %fusion.204 = bf16[1024,2,128]{0,2,1:T(8,128)(2,1)S(1)} fusion(bf16[1024,2,1024]{0,2,1:T(8,128)(2,1)} %convolution_convert_fusion, f32[1024,2,1024]{0,2,1:T(8,128)} %copy-done.1, f32[1024,2]{0,1:T(2,128)S(1)} %log_add_fusion, bf16[1024,1,4,128]{3,0,2,1:T(8,128)(2,1)} %copy-done.95), kind=kOutput, calls=%fused_computation.219 | convolution fusion | flops 556010496 | bytes 25968640 | tf_op jit(solution)/shard_map/kqgt,tke->qkge/dot_general | solution.py:49
  944.1 5.1 fusion.249
  949.3 3.6 convolution_bitcast_fusion
  956.0 4.3 convolution_convert_fusion.2
  960.3 11.4 %fusion.253 = bf16[1024,1,128]{0,2,1:T(8,128)(2,1)} fusion(bf16[1024,2,1024]{0,2,1:T(8,128)(2,1)} %convolution_convert_fusion.2, f32[1024,2,1024]{0,2,1:T(8,128)} %copy-done, f32[1024,2]{0,1:T(2,128)S(1)} %log_add_fusion.2, bf16[1024,1,4,128]{3,0,2,1:T(8,128)(2,1)S(1)} %copy-done.94), kind=kOutput, calls=%fused_computation.244 | convolution fusion | flops 555879424 | bytes 25968640 | tf_op jit(solution)/shard_map/kqgt,qkge->tke/dot_general | solution.py:50
  971.7 12.6 %fusion.206 = bf16[1024,2,128]{0,2,1:T(8,128)(2,1)S(1)} fusion(bf16[1024,2,1024]{0,2,1:T(8,128)(2,1)} %convolution_convert_fusion.2, f32[1024,2,1024]{0,2,1:T(8,128)} %copy-done, f32[1024,2]{0,1:T(2,128)S(1)} %log_add_fusion.2, bf16[1024,1,4,128]{3,0,2,1:T(8,128)(2,1)S(1)} %copy-done.94), kind=kOutput, calls=%fused_computation.221 | convolution fusion | flops 556010496 | bytes 25968640 | tf_op jit(solution)/shard_map/kqgt,tke->qkge/dot_general | solution.py:49
  984.3 5.0 fusion.243
  989.4 3.3 convolution_bitcast_fusion.2
  1039.3 21.6 %psum.7 = f32[2,2,1024]{2,1,0:T(2,128)S(1)} all-reduce(f32[2,2,1024]{2,1,0:T(2,128)S(1)} %pad_maximum_fusion.19), channel_id=1, replica_groups=mesh['dp'=2,'tp'=8] {'tp'}, use_global_device_ids=true, to_apply=%region_52.53 | all-reduce | flops 4096 | bytes 32768 | tf_op jit(solution)/shard_map/psum | solution.py:149
  (480 shorter events, 178.4 us)
Async XLA Ops:
  7.2 6.6 copy-start.53
  7.2 29.8 %all-gather.19.cloned.1.call-start = ((), (), s32[]{:S(2)}) async-start(), calls=%async_computation.16 | async-start | bytes 2359296 | tf_op jit(solution)/shard_map/all_gather | solution.py:78
  12.5 48.2 %all-gather.27.cloned.1.call-start = ((), (), s32[]{:S(2)}) async-start(), calls=%async_computation.24 | async-start | bytes 2359296 | tf_op jit(solution)/shard_map/all_gather | solution.py:78
  13.4 80.9 %reduce-scatter.17.cloned.1.call-start = ((), (), s32[]{:S(2)}) async-start(), calls=%async_computation.17 | async-start | bytes 4718592 | tf_op jit(solution)/shard_map/reduce_scatter | solution.py:86
  13.8 49.9 %copy-start.67 = (pred[1024,1024]{0,1:T(8,128)(4,1)}, pred[1024,1024]{0,1:T(8,128)(4,1)S(1)}, u32[]{:S(2)}) copy-start(pred[1024,1024]{0,1:T(8,128)(4,1)S(1)} %iota_compare_fusion) | copy-start | bytes 3145732
  50.6 10.1 copy-start.72
  50.7 78.5 %reduce-scatter.25.cloned.1.call-start = ((), (), s32[]{:S(2)}) async-start(), calls=%async_computation.25 | async-start | bytes 4718592 | tf_op jit(solution)/shard_map/reduce_scatter | solution.py:86
  74.2 55.0 %copy-start.4 = (bf16[2,128,1024]{2,1,0:T(8,128)(2,1)S(1)}, bf16[2,128,1024]{2,1,0:T(8,128)(2,1)}, u32[]{:S(2)}) copy-start(bf16[2,128,1024]{2,1,0:T(8,128)(2,1)} %param.9) | copy-start | bytes 1572868
  74.3 81.3 %copy-start.7 = (bf16[2,1024,384]{2,1,0:T(8,128)(2,1)S(1)}, bf16[2,1024,384]{2,1,0:T(8,128)(2,1)}, u32[]{:S(2)}) copy-start(bf16[2,1024,384]{2,1,0:T(8,128)(2,1)} %param.15) | copy-start | bytes 4718596
  74.3 81.3 %all-gather.29.cloned.1.call-start = ((), (), s32[]{:S(2)}) async-start(), calls=%async_computation.26 | async-start | bytes 2359296 | tf_op jit(solution)/shard_map/all_gather | solution.py:89
  74.9 83.6 %copy-start.91 = (f32[1,1024]{1,0:T(1,128)}, f32[1,1024]{1,0:T(1,128)S(1)}, u32[]{:S(2)}) copy-start(f32[1,1024]{1,0:T(1,128)S(1)} %get-tuple-element.74) | copy-start | bytes 12292
  130.7 27.9 %copy-start.121 = (f32[128]{0:T(128)}, f32[128]{0:T(128)S(1)}, u32[]{:S(2)}) copy-start(f32[128]{0:T(128)S(1)} %get-tuple-element.67) | copy-start | bytes 1540
  131.2 27.3 %copy-start.111 = (f32[128]{0:T(128)}, f32[128]{0:T(128)S(1)}, u32[]{:S(2)}) copy-start(f32[128]{0:T(128)S(1)} %fusion.421) | copy-start | bytes 1540
  131.2 27.3 %copy-start.113 = (f32[128]{0:T(128)}, f32[128]{0:T(128)S(1)}, u32[]{:S(2)}) copy-start(f32[128]{0:T(128)S(1)} %fusion.425) | copy-start | bytes 1540
  132.3 46.9 %all-gather.21.cloned.1.call-start = ((), (), s32[]{:S(2)}) async-start(), calls=%async_computation.18 | async-start | bytes 2359296 | tf_op jit(solution)/shard_map/all_gather | solution.py:89
  132.9 79.8 %reduce-scatter.27.cloned.1.call-start = ((), (), s32[]{:S(2)}) async-start(), calls=%async_computation.27 | async-start | bytes 4718592 | tf_op jit(solution)/shard_map/reduce_scatter | solution.py:94
  165.3 82.4 %reduce-scatter.19.cloned.1.call-start = ((), (), s32[]{:S(2)}) async-start(), calls=%async_computation.19 | async-start | bytes 4718592 | tf_op jit(solution)/shard_map/reduce_scatter | solution.py:94
  189.0 84.2 %all-gather.23.cloned.1.call-start = ((), (), s32[]{:S(2)}) async-start(), calls=%async_computation.20 | async-start | bytes 2359296 | tf_op jit(solution)/shard_map/all_gather | solution.py:78
  250.0 68.5 %reduce-scatter.21.cloned.1.call-start = ((), (), s32[]{:S(2)}) async-start(), calls=%async_computation.21 | async-start | bytes 4718592 | tf_op jit(solution)/shard_map/reduce_scatter | solution.py:86
  287.1 56.7 %all-gather.31.cloned.1.call-start = ((), (), s32[]{:S(2)}) async-start(), calls=%async_computation.28 | async-start | bytes 2359296 | tf_op jit(solution)/shard_map/all_gather | solution.py:78
  287.9 79.0 %all-gather.47.cloned.1.call-start = ((), (), s32[]{:S(2)}) async-start(), calls=%async_computation.46 | async-start | bytes 2359296 | tf_op jit(solution)/shard_map/all_gather | solution.py:117
  289.0 101.1 %all-gather.25.cloned.1.call-start = ((), (), s32[]{:S(2)}) async-start(), calls=%async_computation.22 | async-start | bytes 2359296 | tf_op jit(solution)/shard_map/all_gather | solution.py:89
  321.2 102.2 %reduce-scatter.29.cloned.1.call-start = ((), (), s32[]{:S(2)}) async-start(), calls=%async_computation.29 | async-start | bytes 4718592 | tf_op jit(solution)/shard_map/reduce_scatter | solution.py:86
  357.4 101.0 %reduce-scatter.33.cloned.1.call-start = ((), (), s32[]{:S(2)}) async-start(), calls=%async_computation.32 | async-start | bytes 4718592 | tf_op jit(solution)/shard_map/reduce_scatter | solution.py:130
  399.8 83.3 %all-gather.49.cloned.1.call-start = ((), (), s32[]{:S(2)}) async-start(), calls=%async_computation.47 | async-start | bytes 2359296 | tf_op jit(solution)/shard_map/all_gather | solution.py:117
  400.4 105.7 %all-gather.33.cloned.1.call-start = ((), (), s32[]{:S(2)}) async-start(), calls=%async_computation.30 | async-start | bytes 2359296 | tf_op jit(solution)/shard_map/all_gather | solution.py:89
  460.6 88.2 %reduce-scatter.41.cloned.1.call-start = ((), (), s32[]{:S(2)}) async-start(), calls=%async_computation.39 | async-start | bytes 4718592 | tf_op jit(solution)/shard_map/reduce_scatter | solution.py:130
  517.5 66.4 %reduce-scatter.23.cloned.1.call-start = ((), (), s32[]{:S(2)}) async-start(), calls=%async_computation.23 | async-start | bytes 4718592 | tf_op jit(solution)/shard_map/reduce_scatter | solution.py:94
  520.9 98.0 %reduce-scatter.31.cloned.1.call-start = ((), (), s32[]{:S(2)}) async-start(), calls=%async_computation.31 | async-start | bytes 4718592 | tf_op jit(solution)/shard_map/reduce_scatter | solution.py:94
  525.5 119.8 %all-gather.41.cloned.1.call-start = ((), (), s32[]{:S(2)}) async-start(), calls=%async_computation.40 | async-start | bytes 2359296 | tf_op jit(solution)/shard_map/all_gather | solution.py:135
  622.0 67.1 %all-gather.35.cloned.1.call-start = ((), (), s32[]{:S(2)}) async-start(), calls=%async_computation.33 | async-start | bytes 2359296 | tf_op jit(solution)/shard_map/all_gather | solution.py:135
  622.8 110.8 %reduce-scatter.43.cloned.1.call-start = ((), (), s32[]{:S(2)}) async-start(), calls=%async_computation.41 | async-start | bytes 4718592 | tf_op jit(solution)/shard_map/reduce_scatter | solution.py:143
  679.3 5.9 copy-start.75
  679.3 5.9 copy-start.139
  679.3 5.9 copy-start.147
  688.9 75.9 %reduce-scatter.35.cloned.1.call-start = ((), (), s32[]{:S(2)}) async-start(), calls=%async_computation.34 | async-start | bytes 4718592 | tf_op jit(solution)/shard_map/reduce_scatter | solution.py:143
  723.9 6.0 copy-start.76
  723.9 6.0 copy-start.137
  723.9 6.0 copy-start.143
  733.5 58.7 %all-gather.43.cloned.1.call-start = ((), (), s32[]{:S(2)}) async-start(), calls=%async_computation.42 | async-start | bytes 2359296 | tf_op jit(solution)/shard_map/all_gather | solution.py:117
  768.9 47.0 %all-gather.37.cloned.1.call-start = ((), (), s32[]{:S(2)}) async-start(), calls=%async_computation.35 | async-start | bytes 2359296 | tf_op jit(solution)/shard_map/all_gather | solution.py:117
  769.6 79.7 %reduce-scatter.45.cloned.1.call-start = ((), (), s32[]{:S(2)}) async-start(), calls=%async_computation.43 | async-start | bytes 4718592 | tf_op jit(solution)/shard_map/reduce_scatter | solution.py:130
  802.3 82.1 %reduce-scatter.37.cloned.1.call-start = ((), (), s32[]{:S(2)}) async-start(), calls=%async_computation.36 | async-start | bytes 4718592 | tf_op jit(solution)/shard_map/reduce_scatter | solution.py:130
  825.6 58.8 %copy-start.92 = (f32[1,1024]{1,0:T(1,128)S(1)}, f32[1,1024]{1,0:T(1,128)}, u32[]{:S(2)}) copy-start(f32[1,1024]{1,0:T(1,128)} %copy-done.91) | copy-start | bytes 12292
  825.6 58.8 %copy-start.112 = (f32[128]{0:T(128)S(1)}, f32[128]{0:T(128)}, u32[]{:S(2)}) copy-start(f32[128]{0:T(128)} %copy-done.111) | copy-start | bytes 1540
  825.6 58.8 %copy-start.114 = (f32[128]{0:T(128)S(1)}, f32[128]{0:T(128)}, u32[]{:S(2)}) copy-start(f32[128]{0:T(128)} %copy-done.113) | copy-start | bytes 1540
  825.6 60.3 %copy-start.122 = (f32[128]{0:T(128)S(1)}, f32[128]{0:T(128)}, u32[]{:S(2)}) copy-start(f32[128]{0:T(128)} %copy-done.121) | copy-start | bytes 1540
  825.6 60.4 %copy-start.120 = (f32[128]{0:T(128)S(1)}, f32[128]{0:T(128)}, u32[]{:S(2)}) copy-start(f32[128]{0:T(128)} %copy-done.119) | copy-start | bytes 1540
  825.6 60.4 %copy-start.48 = (bf16[128,1024]{1,0:T(8,128)(2,1)S(1)}, bf16[128,1024]{1,0:T(8,128)(2,1)}, u32[]{:S(2)}) copy-start(bf16[128,1024]{1,0:T(8,128)(2,1)} %get-tuple-element.81) | copy-start | bytes 786436
  825.6 60.4 %copy-start.49 = (bf16[128,1024]{1,0:T(8,128)(2,1)S(1)}, bf16[128,1024]{1,0:T(8,128)(2,1)}, u32[]{:S(2)}) copy-start(bf16[128,1024]{1,0:T(8,128)(2,1)} %get-tuple-element.82) | copy-start | bytes 786436
  825.7 63.9 %copy-start.103 = (f32[1024,2]{0,1:T(2,128)S(1)}, f32[1024,2]{0,1:T(2,128)}, u32[]{:S(2)}) copy-start(f32[1024,2]{0,1:T(2,128)} %copy-done.102) | copy-start | bytes 24580
  825.7 63.9 %copy-start.105 = (f32[1024,2]{0,1:T(2,128)S(1)}, f32[1024,2]{0,1:T(2,128)}, u32[]{:S(2)}) copy-start(f32[1024,2]{0,1:T(2,128)} %copy-done.104) | copy-start | bytes 24580
  825.7 86.0 %copy-start.29 = (bf16[2,2,128,1024]{3,2,1,0:T(8,128)(2,1)S(1)}, bf16[2,2,128,1024]{3,2,1,0:T(8,128)(2,1)}, u32[]{:S(2)}) copy-start(bf16[2,2,128,1024]{3,2,1,0:T(8,128)(2,1)} %param.14) | copy-start | bytes 3145732
  825.7 86.0 %all-gather.45.cloned.1.call-start = ((), (), s32[]{:S(2)}) async-start(), calls=%async_computation.44 | async-start | bytes 2359296 | tf_op jit(solution)/shard_map/all_gather | solution.py:135
  888.4 65.2 %all-gather.39.cloned.1.call-start = ((), (), s32[]{:S(2)}) async-start(), calls=%async_computation.37 | async-start | bytes 2359296 | tf_op jit(solution)/shard_map/all_gather | solution.py:135
  889.1 148.5 %reduce-scatter.47.cloned.1.call-start = ((), (), s32[]{:S(2)}) async-start(), calls=%async_computation.45 | async-start | bytes 4718592 | tf_op jit(solution)/shard_map/reduce_scatter | solution.py:143
  944.1 5.2 copy-start.141
  952.9 84.6 %reduce-scatter.39.cloned.1.call-start = ((), (), s32[]{:S(2)}) async-start(), calls=%async_computation.38 | async-start | bytes 4718592 | tf_op jit(solution)/shard_map/reduce_scatter | solution.py:143
  1036.4 25.1 %copy-start.116 = (f32[128]{0:T(128)S(1)}, f32[128]{0:T(128)}, u32[]{:S(2)}) copy-start(f32[128]{0:T(128)} %copy-done.115) | copy-start | bytes 1540
  1036.4 25.1 %copy-start.118 = (f32[128]{0:T(128)S(1)}, f32[128]{0:T(128)}, u32[]{:S(2)}) copy-start(f32[128]{0:T(128)} %copy-done.117) | copy-start | bytes 1540
  1036.5 25.1 %copy-start.46 = (bf16[128,1024]{1,0:T(8,128)(2,1)S(1)}, bf16[128,1024]{1,0:T(8,128)(2,1)}, u32[]{:S(2)}) copy-start(bf16[128,1024]{1,0:T(8,128)(2,1)} %get-tuple-element.77) | copy-start | bytes 786436
  1036.5 25.1 %copy-start.47 = (bf16[128,1024]{1,0:T(8,128)(2,1)S(1)}, bf16[128,1024]{1,0:T(8,128)(2,1)}, u32[]{:S(2)}) copy-start(bf16[128,1024]{1,0:T(8,128)(2,1)} %get-tuple-element.78) | copy-start | bytes 786436
  1037.5 24.0 %copy-start.60 = (f32[128,1024]{1,0:T(8,128)S(1)}, f32[128,1024]{1,0:T(8,128)}, u32[]{:S(2)}) copy-start(f32[128,1024]{1,0:T(8,128)} %reduce-scatter.47.cloned.1.call-done) | copy-start | bytes 1572868
  1037.6 24.0 %copy-start.61 = (f32[128,1024]{1,0:T(8,128)S(1)}, f32[128,1024]{1,0:T(8,128)}, u32[]{:S(2)}) copy-start(f32[128,1024]{1,0:T(8,128)} %reduce-scatter.39.cloned.1.call-done) | copy-start | bytes 1572868
  (119 other events, 258.0 us)
Sparse Core Ops, SparseCore 0:
  12.7 24.2 all-gather.18
  39.2 21.5 all-gather.26
  63.1 31.1 reduce-scatter.16
  96.5 32.7 reduce-scatter.24
  132.4 23.1 all-gather.28
  157.6 21.5 all-gather.20
  181.5 31.1 reduce-scatter.26
  215.0 32.6 reduce-scatter.18
  250.1 23.0 all-gather.22
  287.2 31.1 reduce-scatter.20
  320.6 23.1 all-gather.30
  345.3 21.5 all-gather.46
  368.5 21.5 all-gather.24
  392.2 31.1 reduce-scatter.28
  425.6 32.7 reduce-scatter.32
  459.9 23.1 all-gather.48
  484.5 21.5 all-gather.32
  517.6 31.1 reduce-scatter.40
  551.1 32.7 reduce-scatter.22
  586.0 32.7 reduce-scatter.30
  622.1 23.1 all-gather.40
  647.5 21.5 all-gather.34
  689.0 31.1 reduce-scatter.42
  733.6 31.1 reduce-scatter.34
  769.0 23.1 all-gather.42
  794.3 21.5 all-gather.36
  818.0 31.1 reduce-scatter.44
  851.6 32.7 reduce-scatter.36
  888.5 23.1 all-gather.44
  913.1 21.5 all-gather.38
  953.1 31.1 reduce-scatter.46
  992.9 31.1 reduce-scatter.38
where the time goes:
time: 1080 us; the launch traced here: 1070 us
  waiting for transfers between devices  648 us (60%)
  matrix products  298 us (28%)
  local copies, waits for them, and re-layouts  41.3 us (4%)
  other arithmetic  40.9 us (4%)
  blocking collectives  21.6 us (2%)
  between operations  16.4 us (2%)
    reduce_scatter x4, waiting for transfers between devices, device_program(): lax.psum_scatter(down_part, 'tp', scatter_dimension=0, tiled=True)  126 us
    reduce_scatter x4, waiting for transfers between devices, device_program(): lax.psum_scatter(grad_nb_part, 'tp', scatter_dimension=0, tiled=True)  115 us
    reduce_scatter x4, waiting for transfers between devices, device_program(): lax.psum_scatter(attn_part, 'tp', scatter_dimension=0, tiled=True)  107 us
    all_gather x4, waiting for transfers between devices, device_program(): normed_full = lax.all_gather(normed, 'tp', axis=0, tiled=True)  76.4 us
    all_gather x4, waiting for transfers between devices, device_program(): normed_b_full = lax.all_gather(normed_b, 'tp', axis=0, tiled=True)  74.7 us
    all_gather x4, waiting for transfers between devices, device_program(): grad_full = lax.all_gather(grad_in, 'tp', axis=0, tiled=True)  67.9 us
    dot_general x4, matrix products, attention_backward(): jnp.einsum('kqgt,tke->qkge', grad_scores, key_heads, preferred_element_ty...  52.3 us
    dot_general x4, matrix products, attention_backward(): jnp.einsum('kqgt,qkge->tke', grad_scores, queries, preferred_element_type...  51.7 us
  transfers between devices with their start and end apart: 32, of which 27 were waited for; matrix products, arithmetic and copies ran while one was open for 28% of the time, Pallas kernels for 0%

commit v1 on v0

v1 whole, which is shorter than its diff:
```python
import functools

import jax
import jax.numpy as jnp
from jax import lax
from jax.experimental import pallas as pl
from jax.experimental.pallas import tpu as pltpu
from jax.sharding import PartitionSpec as P

NORM_EPS = 1e-5
MESH = pl.DeviceIdType.MESH
BF16 = jnp.bfloat16
F32 = jnp.float32
VMEM_BYTES = 67043328
HEAD = 128
SPLITS = ()

(XR, UR, HR, VR, YR, GR, FN, FS, PREC, RFU, RFD, RU, RD, SA, SB, QKV, MIX, LSE, GP,
 WQ, WO, W1, W3, W2, GA, GM, AQ, AO, A1, A3, A2, BQ, BO, B1, B3, B2, PART, DQKV, DK, DV, GBUF, GSUM) = range(42)


def dot_nn(a, b):
    return lax.dot_general(a, b, (((1,), (0,)), ((), ())), preferred_element_type=F32)


def dot_nt(a, b):
    return lax.dot_general(a, b, (((1,), (1,)), ((), ())), preferred_element_type=F32)


def dot_tn(a, b):
    return lax.dot_general(a, b, (((0,), (0,)), ((), ())), preferred_element_type=F32)


def norm_rows(rows, gain):
    return rows * lax.rsqrt(jnp.mean(rows * rows, axis=-1, keepdims=True) + NORM_EPS) * gain


class Plan:
    def __init__(self, count, micro, layers, rows, width, qkv_w, mix_w, ff):
        self.count, self.micro, self.layers, self.rows, self.width = count, micro, layers, rows, width
        self.qkv_w, self.mix_w, self.ff = qkv_w, mix_w, ff
        self.chips = count // 2
        self.steps = 4 * layers
        self.seq = [(m, k) for k in range(self.steps + 1) for m in range(micro)]

    def shape(self, key):
        kind = key[0]
        c, r, w = self.chips, self.rows, self.width
        if kind in (XR, UR, HR, VR, YR, GR):
            return (r, w), BF16
        if kind in (FN, FS):
            return (c, 2 * r, w), BF16
        if kind == PREC:
            return (c, r, w), F32
        if kind == PART:
            return (c, 2 * r, w), F32
        if kind in (RFU, RFD, SA, SB):
            return (r // 2, w), F32
        if kind in (RU, RD):
            return (r, w), F32
        if kind in (QKV, DQKV):
            return (c, 2 * r, self.qkv_w), BF16
        if kind == MIX:
            return (c, 2 * r, self.mix_w), BF16
        if kind == LSE:
            return (c, self.mix_w // HEAD, 2 * r), F32
        if kind in (GP, GSUM):
            return (2 * self.layers, w), F32
        if kind == GBUF:
            return (self.count, 2 * self.layers, w), F32
        if kind in (GA, GM):
            return (1, w), F32
        if kind in (DK, DV):
            return (2 * c * r, HEAD), F32
        dims = {WQ: (w, self.qkv_w), WO: (self.mix_w, w), W1: (w, self.ff), W3: (w, self.ff), W2: (self.ff, w)}
        for group, dtype in (((WQ, WO, W1, W3, W2), BF16), ((AQ, AO, A1, A3, A2), F32), ((BQ, BO, B1, B3, B2), BF16)):
            if kind in group:
                return dims[WQ + group.index(kind)], dtype
        raise ValueError(kind)

    def comm_of(self, m, k):
        top = 2 * self.layers
        if k == 0:
            return None, None, None, None, None, None, None, ((UR, m, 0, FS),)
        if k < top:
            l = k // 2
            if k % 2:
                return 0, (XR, m, l), None, (GM, l), (HR, m, l), (VR, m, l), None, ()
            return 0, (HR, m, l - 1), None, (GA, l), (XR, m, l), (UR, m, l), None, ()
        if k == top:
            l = self.layers - 1
            return 1, (HR, m, l), None, None, (YR, m), None, None, ((VR, m, l, FS),)
        j = k - top
        l = self.layers - 1 - (j - 1) // 2
        if j % 2:
            return 2, (GR, m), (HR, m, l), (GM, l), (GR, m), None, self.layers + l, ((UR, m, l, FS),)
        sv = () if k == self.steps else ((VR, m, l - 1, FS),)
        return 2, (GR, m), (XR, m, l), (GA, l), (GR, m), None, l, sv

    def comp_of(self, m, k):
        top = 2 * self.layers
        if k < top:
            return (k % 2), k // 2
        return 2 + (k - top) % 2, self.layers - 1 - (k - top) // 2

    def products(self, n):
        if n == 0 or self.seq[n - 1][1] == self.steps:
            return None
        m, k = self.seq[n - 1]
        return (m, k) + self.comp_of(m, k)

    def uses(self, n):
        m, k = self.seq[n]
        ops = []
        kind, base, srow, gain, new, norm, slot, saved = self.comm_of(m, k)
        reads = [sv[:3] for sv in saved]
        writes = [(sv[3], m) for sv in saved]
        if kind is not None:
            reads += [(PREC, m), (RFU, m), (RFD, m), base] + [x for x in (srow, gain) if x]
            if slot is not None:
                reads.append((GP,))
                writes.append((GP,))
            writes += [x for x in (new, norm) if x]
            if kind == 1:
                reads.append((GR, m))
            if k < self.steps:
                writes.append((FN, m))
        if self.products(n):
            pm, pk, comp, l = self.products(n)
            reads += [(FS, pm)] if (comp >= 2 or pk == 0) else [(FN, pm)]
            reads += [(WQ, l), (WO, l)] if comp in (0, 3) else [(W1, l), (W3, l), (W2, l)]
            if comp >= 2:
                reads.append((FN, pm))
                acc = [(AQ,), (AO,)] if comp == 3 else [(A1,), (A3,), (A2,)]
                if pm > 0:
                    reads += acc
                writes += acc
            if comp == 3:
                reads += [(QKV, pm, l), (MIX, pm, l), (LSE, pm, l)]
            if comp == 0:
                writes += [(QKV, pm, l), (MIX, pm, l), (LSE, pm, l)]
            writes += [(PREC, pm), (RFU, pm), (RFD, pm)]
        return reads, writes

    def scratch(self, n):
        m, k = self.seq[n]
        kind = self.comm_of(m, k)[0]
        keys = []
        if kind is not None:
            keys += [(x, m) for x in (RU, RD, SA, SB)]
        if self.products(n):
            comp = self.products(n)[2]
            keys.append((PART,))
            if comp == 3:
                keys += [(DQKV,), (DK,), (DV,), (BQ,), (BO,)]
            if comp == 2:
                keys += [(B1,), (B3,), (B2,)]
        if n == len(self.seq) - 1:
            keys += [(GBUF,), (GSUM,)]
        return keys


class Kernel:
    def __init__(self, plan, cid, first, last):
        self.plan, self.cid, self.first, self.last = plan, cid, first, last
        written, self.live_in, keys = set(), [], []
        for n in range(first, last):
            reads, writes = plan.uses(n)
            for key in reads:
                if key not in written and key not in self.live_in and key != (GP,):
                    self.live_in.append(key)
            if (GP,) in reads and (GP,) not in written and n > 0 and any((GP,) in plan.uses(q)[1] for q in range(first)):
                if (GP,) not in self.live_in:
                    self.live_in.append((GP,))
            written |= set(writes)
            for key in reads + writes + plan.scratch(n):
                if key not in keys:
                    keys.append(key)
        later, seen = [], set()
        for n in range(last, len(plan.seq)):
            reads, writes = plan.uses(n)
            later += [key for key in reads if key in written and key not in seen and key not in later]
            seen |= set(writes)
        self.keys, self.live_out = keys, later
        self.zero_gp = (GP,) in keys and (GP,) not in self.live_in
        self.results = []
        for n in range(first, last):
            m, k = plan.seq[n]
            if k == 2 * plan.layers:
                self.results.append((YR, m))
            if k == plan.steps:
                self.results.append((GR, m))
            if plan.products(n):
                pm, pk, comp, l = plan.products(n)
                if pm == plan.micro - 1 and comp >= 2:
                    self.results += [(x, l) for x in ((BQ, BO) if comp == 3 else (B1, B3, B2))]
            if n == len(plan.seq) - 1:
                self.results.append((GSUM,))

    def out_shape(self, key):
        return jax.ShapeDtypeStruct(*self.plan.shape(key))

    def body(self, *refs):
        pn = self.plan
        ni, no, lo_ = len(self.live_in), len(self.live_out), len(self.results)
        ins = dict(zip(self.live_in, refs[:ni]))
        outs = dict(zip(self.live_out, refs[ni:ni + no]))
        res = dict(zip(self.results, refs[ni + no:ni + no + lo_]))
        s = dict(zip(self.keys, refs[ni + no + lo_:-5]))
        lsem, ssem, rsem, psem, qsem = refs[-5:]
        rows, chips, count = pn.rows, pn.chips, pn.count
        me = lax.axis_index('tp')
        chip, core = lax.div(me, 2), lax.rem(me, 2)
        oc = 1 - core
        cu, cd, cf = lax.rem(chip + 1, chips), lax.rem(chip + chips - 1, chips), lax.rem(chip + 2, chips)
        up, dn, sib = cu * 2 + core, cd * 2 + core, chip * 2 + oc
        final = self.last == len(pn.seq)
        nloc = [0]
        sent = [[] for _ in range(pn.micro)]

        def local(a, b):
            d = pltpu.make_async_copy(a, b, lsem.at[nloc[0]])
            nloc[0] += 1
            d.start()
            return d

        def remote(a, b, dev, m, slot, keep=True):
            d = pltpu.make_async_remote_copy(src_ref=a, dst_ref=b, send_sem=ssem.at[m, slot], recv_sem=rsem.at[m, slot],
                                             device_id={'tp': dev}, device_id_type=MESH)
            if keep:
                sent[m].append(d)
            return d

        def blk(ref, c, k, lo=0, size=rows):
            return ref.at[c, pl.ds(pl.multiple_of(k * rows + lo, 16), size)]

        barrier = pltpu.get_barrier_semaphore()
        peers = [lax.rem(me + off, count) for off in range(1, count)] if final else [up, dn, sib]
        for dev in peers:
            pl.semaphore_signal(barrier, inc=1, device_id={'tp': dev}, device_id_type=MESH)
        loads = {key: local(ins[key], s[key]) for key in self.live_in}
        stores = {}

        def need(*keys):
            for key in keys:
                if key in loads:
                    loads.pop(key).wait()

        def store(key, src, dst):
            stores[key] = local(src, dst)

        if self.zero_gp:
            s[(GP,)][...] = jnp.zeros_like(s[(GP,)])
        pl.semaphore_wait(barrier, len(peers))

        h2, h4 = rows // 2, rows // 4
        halves = range(2)
        far = [None] * pn.micro
        open_gathers = []

        def rs_far(m):
            red = s[(PREC, m)]
            far[m] = []
            for h in halves:
                lo = h * h2
                far[m].append((remote(red.at[cf, pl.ds(lo, h4)], s[(RFU, m)].at[pl.ds(h * h4, h4)], up, m, 4 * h, False),
                               remote(red.at[cf, pl.ds(lo + h4, h4)], s[(RFD, m)].at[pl.ds(h * h4, h4)], dn, m, 4 * h + 1, False)))
                for d in far[m][h]:
                    d.start()

        def rs_mid(m):
            need((PREC, m), (RFU, m), (RFD, m))
            red, dep, ind = s[(PREC, m)], [], []
            for h in halves:
                lo, q = h * h2, pl.ds(h * h4, h4)
                if far[m]:
                    for d in far[m][h]:
                        d.wait_recv()
                s[(SA, m)][q] = red[cu, pl.ds(lo, h4)] + s[(RFU, m)][q]
                s[(SB, m)][q] = red[cd, pl.ds(lo + h4, h4)] + s[(RFD, m)][q]
                dep.append((remote(s[(SA, m)].at[q], s[(RU, m)].at[pl.ds(lo, h4)], up, m, 4 * h + 2),
                            remote(s[(SB, m)].at[q], s[(RD, m)].at[pl.ds(lo + h4, h4)], dn, m, 4 * h + 3)))
                for d in dep[h]:
                    d.start()
            drain = [d for pair in far[m] or [] for d in pair]
            far[m] = None
            for h in halves:
                lo = h * h2
                ind.append((remote(red.at[cu, pl.ds(lo + h4, h4)], s[(RU, m)].at[pl.ds(lo + h4, h4)], up, m, 8 + 2 * h, False),
                            remote(red.at[cd, pl.ds(lo, h4)], s[(RD, m)].at[pl.ds(lo, h4)], dn, m, 9 + 2 * h, False)))
                for d in ind[h]:
                    d.start()
            return [dep[h] + ind[h] for h in halves], drain + [d for pair in ind for d in pair]

        def ag_make(full, m, lo, size, slot):
            own = blk(full, chip, core, lo, size)
            return [remote(own, own, up, m, slot), remote(own, own, dn, m, slot + 1), remote(own, own, sib, m, slot + 2)]

        def ag_mid(full, m, lo, size, slot, st):
            a = size // 2
            st[0].wait_recv()
            fa = blk(full, cd, core, lo, a)
            st.append(remote(fa, fa, up, m, slot + 3))
            st[3].start()
            st[1].wait_recv()
            fb = blk(full, cu, core, lo + a, a)
            st.append(remote(fb, fb, dn, m, slot + 4))
            st[4].start()
            for q, c in enumerate((cd, cu)):
                r = blk(full, c, core, lo, size)
                st.append(remote(r, r, sib, m, slot + 5 + q))
                st[5 + q].start()

        def ag_far(full, m, lo, size, slot, st):
            st[3].wait_recv()
            st[4].wait_recv()
            r = blk(full, cf, core, lo, size)
            st.append(remote(r, r, sib, m, slot + 7))
            st[7].start()

        def ag_end(full, m, lo, size, slot, st):
            for q in (2, 5, 6, 7):
                st[q].wait_recv()

        def close():
            for g in open_gathers:
                ag_far(*g)
            for g in open_gathers:
                ag_end(*g)
            for g in open_gathers:
                for d in sent[g[1]]:
                    d.wait_send()
                sent[g[1]].clear()
            open_gathers.clear()

        def part_copy(m, t):
            return pltpu.make_async_remote_copy(
                src_ref=s[(PART,)].at[t, pl.ds(pl.multiple_of(oc * rows, 16), rows)], dst_ref=s[(PREC, m)].at[t],
                send_sem=psem.at[m, t], recv_sem=qsem.at[m, t], device_id={'tp': sib}, device_id_type=MESH)

        def loop(fn, m=None, hook=None, at=0):
            def step(t, carry):
                fn(t)
                if m is not None:
                    @pl.when(t > 0)
                    def _():
                        part_copy(m, t - 1).start()
                if hook is not None:
                    @pl.when(t == at)
                    def _():
                        hook()
                return carry
            lax.fori_loop(0, chips, step, 0)
            if m is not None:
                part_copy(m, chips - 1).start()


        for n in range(self.first, self.last):
            m, k = pn.seq[n]
            kind, base, srow, gain, new, norm, slot, saved = pn.comm_of(m, k)
            gathers = []
            arrive, drain = rs_mid(m) if kind is not None else (None, None)
            for q, sv in enumerate(saved):
                key = sv[:3]
                need(key)
                full = s[(sv[3], m)]
                full[chip, pl.ds(pl.multiple_of(core * rows, 16), rows)] = s[key][...]
                st = ag_make(full, m, 0, rows, 12 + 8 * q)
                for d in st:
                    d.start()
                gathers.append((full, m, 0, rows, 12 + 8 * q, st))
            close()

            hook = None
            if kind is not None:
                need(*[x for x in (base, srow, gain) if x])
                if slot is not None:
                    need((GP,))
                news = []
                if kind == 1:
                    need((GR, m))
                if k < pn.steps:
                    full = s[(FN, m)]
                    news = [(full, m, h * h2, h2, 28 + 8 * h, ag_make(full, m, h * h2, h2, 28 + 8 * h)) for h in halves]
                starts = [pl.multiple_of(core * rows + h * h2, 16) for h in halves]
                hook = functools.partial(self.rows_step, s, m, kind, base, srow, gain, new, norm, slot, arrive, drain, news, starts, chip, h2)

            if pn.products(n):
                pm, pk, comp, l = pn.products(n)
                full = s[(FS, pm)] if (comp >= 2 or pk == 0) else s[(FN, pm)]
                need((FS, pm), (FN, pm))
                fn = (self.attn_f, self.mlp_f, self.mlp_b, self.attn_b)[comp]
                for x in ((BQ, BO) if comp == 3 else (B1, B3, B2) if comp == 2 else ()):
                    if (x, l + 1) in stores:
                        stores.pop((x, l + 1)).wait()
                fn(s, need, loop, hook, pm, l, full)
                red = s[(PREC, pm)]
                for c in range(chips):
                    d = part_copy(pm, c)
                    d.wait_recv()
                    red[c] = red[c] + s[(PART,)][c, pl.ds(pl.multiple_of(core * rows, 16), rows)]
                    d.wait_send()
                rs_far(pm)
                if comp >= 2 and pm == pn.micro - 1:
                    for a, b in ((AQ, BQ), (AO, BO)) if comp == 3 else ((A1, B1), (A3, B3), (A2, B2)):
                        s[(b,)][...] = s[(a,)][...].astype(BF16)
                        store((b, l), s[(b,)], res[(b, l)])
            elif hook is not None:
                hook()

            if kind is not None:
                gathers += news
            if new is not None and new in res and (new[0] == YR or k == pn.steps):
                store(new, s[new], res[new])
            for g in gathers:
                ag_mid(*g)
            open_gathers.extend(gathers)

        close()
        if final:
            gb = s[(GBUF,)]
            gb[me] = s[(GP,)][...]
            gs = [remote(gb.at[me], gb.at[me], lax.rem(me + off, count), 0, 43 + off) for off in range(1, count)]
            for d in gs:
                d.start()
            for d in gs:
                d.wait_recv()
            acc = gb[0]
            for q in range(1, count):
                acc = acc + gb[q]
            s[(GSUM,)][...] = acc
            store((GSUM,), s[(GSUM,)], res[(GSUM,)])
        for m in range(pn.micro):
            if far[m]:
                for pair in far[m]:
                    for d in pair:
                        d.wait_recv()
                        d.wait_send()
            for d in sent[m]:
                d.wait_send()
        for key in self.live_out:
            need(key)
            store((key,), s[key], outs[key])
        for d in stores.values():
            d.wait()
        assert not loads

    def rows_step(self, s, m, kind, base, srow, gain, new, norm, slot, arrive, drain, news, starts, chip, h2):
        red, ru, rd = s[(PREC, m)], s[(RU, m)], s[(RD, m)]
        for h in range(2):
            for d in arrive[h]:
                d.wait_recv()
            q = pl.ds(h * h2, h2)
            total = (red[chip, q] + ru[q] + rd[q]).astype(BF16).astype(F32)
            if kind == 2:
                x = s[srow][q].astype(F32)
                scale = lax.rsqrt(jnp.mean(x * x, axis=-1, keepdims=True) + NORM_EPS)
                s[(GP,)][slot:slot + 1] += jnp.sum(total * x * scale, axis=0, keepdims=True)
                ct = total * s[gain][...]
                total = scale * ct - x * (scale * scale * scale) * jnp.mean(ct * x, axis=-1, keepdims=True)
            val = (s[base][q].astype(F32) + total).astype(BF16)
            s[new][q] = val
            if kind == 0:
                val = norm_rows(val.astype(F32), s[gain][...]).astype(BF16)
                s[norm][q] = val
            if kind == 1:
                val = s[(GR, m)][q]
            if h == 1:
                for d in drain:
                    d.wait_send()
            if news:
                s[(FN, m)][chip, pl.ds(starts[h], h2)] = val
                for d in news[h][5]:
                    d.start()

    def scores(self, t, keys, q):
        total, rows2 = keys.shape[0], q.shape[0]
        sc = dot_nt(keys, q) * HEAD ** -0.5
        kpos = lax.broadcasted_iota(jnp.int32, (total, rows2), 0)
        qpos = lax.broadcasted_iota(jnp.int32, (total, rows2), 1) + t * rows2
        return jnp.where(kpos <= qpos, sc, -1e30)

    def heads(self, qkv):
        ow, total = self.plan.mix_w, 2 * self.plan.chips * self.plan.rows
        return (qkv[:, :, ow:ow + HEAD].reshape(total, HEAD), qkv[:, :, ow + HEAD:ow + 2 * HEAD].reshape(total, HEAD))

    def attn_f(self, s, need, loop, hook, m, l, full):
        need((WQ, l), (WO, l))
        qkv, mix, lse = s[(QKV, m, l)], s[(MIX, m, l)], s[(LSE, m, l)]

        def proj(t):
            qkv[t] = dot_nn(full[t], s[(WQ, l)][...]).astype(BF16)
        loop(proj)

        def attend(t):
            keys, vals = self.heads(qkv)
            for h in range(self.plan.mix_w // HEAD):
                cols = slice(h * HEAD, (h + 1) * HEAD)
                sc = self.scores(t, keys, qkv[t, :, cols])
                top = jnp.max(sc, axis=0, keepdims=True)
                ex = jnp.exp(sc - top)
                tot = jnp.sum(ex, axis=0, keepdims=True)
                lse[t, h:h + 1] = top + jnp.log(tot)
                mix[t, :, cols] = dot_tn((ex * (1.0 / tot)).astype(BF16), vals).astype(BF16)
            s[(PART,)][t] = dot_nn(mix[t], s[(WO, l)][...])
        loop(attend, m, hook, 1)

    def mlp_f(self, s, need, loop, hook, m, l, full):
        need((W1, l), (W3, l), (W2, l))

        def tile(t):
            v = full[t]
            g = dot_nn(v, s[(W1, l)][...])
            w = dot_nn(v, s[(W3, l)][...])
            s[(PART,)][t] = dot_nn((g * jax.nn.sigmoid(g) * w).astype(BF16), s[(W2, l)][...])
        loop(tile, m)
        if hook is not None:
            hook()

    def start_sums(self, s, need, m, keys):
        for key in keys:
            if m > 0:
                need(key)
            else:
                s[key][...] = jnp.zeros_like(s[key])

    def mlp_b(self, s, need, loop, hook, m, l, full):
        need((W1, l), (W3, l), (W2, l))
        self.start_sums(s, need, m, ((A1,), (A3,), (A2,)))
        grad = s[(FN, m)]

        def tile(t):
            v, dy = full[t], grad[t]
            g = dot_nn(v, s[(W1, l)][...])
            w = dot_nn(v, s[(W3, l)][...])
            sig = jax.nn.sigmoid(g)
            act = g * sig
            s[(A2,)][...] += dot_tn((act * w).astype(BF16), dy)
            dm = dot_nt(dy, s[(W2, l)][...]).astype(BF16).astype(F32)
            dw = (dm * act).astype(BF16)
            dg = (dm * w * sig * (1.0 + g * (1.0 - sig))).astype(BF16)
            s[(A1,)][...] += dot_tn(v, dg)
            s[(A3,)][...] += dot_tn(v, dw)
            s[(PART,)][t] = dot_nt(dg, s[(W1, l)][...]) + dot_nt(dw, s[(W3, l)][...])
        loop(tile, m, hook, 2)

    def attn_b(self, s, need, loop, hook, m, l, full):
        need((WQ, l), (WO, l), (QKV, m, l), (MIX, m, l), (LSE, m, l))
        self.start_sums(s, need, m, ((AQ,), (AO,)))
        grad, dqkv, dk, dv = s[(FN, m)], s[(DQKV,)], s[(DK,)], s[(DV,)]
        qkv, mix, lse = s[(QKV, m, l)], s[(MIX, m, l)], s[(LSE, m, l)]
        dk[...] = jnp.zeros_like(dk)
        dv[...] = jnp.zeros_like(dv)

        def attend(t):
            dh = grad[t]
            s[(AO,)][...] += dot_tn(mix[t], dh)
            do = dot_nt(dh, s[(WO, l)][...]).astype(BF16)
            keys, vals = self.heads(qkv)
            for h in range(self.plan.mix_w // HEAD):
                cols = slice(h * HEAD, (h + 1) * HEAD)
                q, doh = qkv[t, :, cols], do[:, cols]
                prob = jnp.exp(self.scores(t, keys, q) - lse[t, h:h + 1])
                dv[...] += dot_nn(prob.astype(BF16), doh)
                dp = dot_nt(vals, doh).astype(BF16).astype(F32)
                rd = jnp.sum(dp * prob, axis=0, keepdims=True)
                ds = (prob * (dp - rd) * HEAD ** -0.5).astype(BF16)
                dk[...] += dot_nn(ds, q)
                dqkv[t, :, cols] = dot_tn(ds, keys).astype(BF16)
        loop(attend, None, hook, 2)
        ow, shp = self.plan.mix_w, dqkv.shape[:2] + (HEAD,)
        dqkv[:, :, ow:ow + HEAD] = dk[...].astype(BF16).reshape(shp)
        dqkv[:, :, ow + HEAD:ow + 2 * HEAD] = dv[...].astype(BF16).reshape(shp)

        def tile(t):
            s[(AQ,)][...] += dot_tn(full[t], dqkv[t])
            s[(PART,)][t] = dot_nt(dqkv[t], s[(WQ, l)][...])
        loop(tile, m)

    def run(self, state):
        any_spec = pl.BlockSpec(memory_space=pl.ANY)
        out_keys = self.live_out + self.results
        pn = self.plan
        vals = pl.pallas_call(
            self.body,
            out_shape=[self.out_shape((key[0],)) if key[0] in (BQ, BO, B1, B3, B2) else self.out_shape(key) for key in out_keys],
            in_specs=[any_spec] * len(self.live_in),
            out_specs=[any_spec] * len(out_keys),
            scratch_shapes=[pltpu.VMEM(*pn.shape(key)) for key in self.keys] + [
                pltpu.SemaphoreType.DMA((len(self.live_in) + len(out_keys),)),
                pltpu.SemaphoreType.DMA((pn.micro, 52)), pltpu.SemaphoreType.DMA((pn.micro, 52)),
                pltpu.SemaphoreType.DMA((pn.micro, pn.chips)), pltpu.SemaphoreType.DMA((pn.micro, pn.chips))],
            compiler_params=pltpu.CompilerParams(collective_id=self.cid, has_side_effects=True, vmem_limit_bytes=VMEM_BYTES),
        )(*[state[key] for key in self.live_in])
        state.update(zip(out_keys, vals))


def solution(mesh):
    rows_p = P(None, ('dp', 'tp'), None)
    flat = P(None, None)
    cols_p = P(None, None, 'tp')
    head_p = P(None, 'tp', None, None)
    down_p = P(None, 'tp', None)
    count = mesh.shape['tp']

    def device_program(x_in, y_cot, gain_attn, gain_mlp, w_qkv, w_out, w_gate, w_up, w_down):
        micro, rows, width = x_in.shape
        layers = w_qkv.shape[0]
        wq = w_qkv.reshape(layers, width, -1)
        wo = w_out.reshape(layers, -1, width)
        plan = Plan(count, micro, layers, rows, width, wq.shape[2], wo.shape[1], w_gate.shape[2])
        state = {}
        for m in range(micro):
            state[(XR, m, 0)] = x_in[m]
            state[(GR, m)] = y_cot[m]
            state[(UR, m, 0)] = norm_rows(x_in[m].astype(F32), gain_attn[0:1]).astype(BF16)
        for l in range(layers):
            for key, arr in ((WQ, wq), (WO, wo), (W1, w_gate), (W3, w_up), (W2, w_down)):
                state[(key, l)] = arr[l]
            state[(GA, l)], state[(GM, l)] = gain_attn[l:l + 1], gain_mlp[l:l + 1]
        cuts = [0] + list(SPLITS) + [len(plan.seq)]
        for cid in range(len(cuts) - 1):
            Kernel(plan, cid, cuts[cid], cuts[cid + 1]).run(state)

        def stack(key, shape):
            return jnp.stack([state[(key, l)].reshape(shape) for l in range(layers)])

        gsum = state[(GSUM,)]
        return (jnp.stack([state[(YR, m)] for m in range(micro)]), jnp.stack([state[(GR, m)] for m in range(micro)]),
                stack(BQ, w_qkv.shape[1:]), stack(BO, w_out.shape[1:]), stack(B1, w_gate.shape[1:]),
                stack(B3, w_up.shape[1:]), stack(B2, w_down.shape[1:]), gsum[:layers], gsum[layers:])

    return jax.shard_map(device_program, mesh=mesh,
                         in_specs=(rows_p, rows_p, flat, flat, P(None, None, 'tp', None, None), head_p, cols_p, cols_p, down_p),
                         out_specs=(rows_p, rows_p, P('dp', None, 'tp', None, None), P('dp', 'tp', None, None), P('dp', None, 'tp'),
                                    P('dp', None, 'tp'), P('dp', 'tp', None), P('dp', None), P('dp', None)),
                         check_vma=False)
```

time: 1080 us -> 562 us (0.52)
  waiting for transfers between devices: 648 us -> 0 us
  Pallas kernels: 0 us -> 528 us
  matrix products: 298 us -> 0 us
  local copies, waits for them, and re-layouts: 41.3 us -> 15.3 us
  other arithmetic: 40.9 us -> 15.2 us
  blocking collectives: 21.6 us -> 0 us
  between operations: 16.4 us -> 0.99 us
    pallas_call x0 -> x1, Pallas kernels: none -> 528 us  [run(): pl.pallas_call(self.body, out_shape=[self.out_shape((key[0],)) if key[0]...]
    reduce_scatter x16 -> x0, waiting for transfers between devices: 379 us -> none  [the longest x4 126 us: device_program(): lax.psum_scatter(down_part, 'tp', scatter_dimension=0, tiled=True)]
    dot_general x84 -> x0, matrix products: 298 us -> none  [the longest x4 52.3 us: attention_backward(): jnp.einsum('kqgt,tke->qkge', grad_scores, key_heads, preferred_element_ty...]
    all_gather x16 -> x0, waiting for transfers between devices: 263 us -> none  [the longest x4 76.4 us: device_program(): normed_full = lax.all_gather(normed, 'tp', axis=0, tiled=True)]
    unnamed x303 -> x36, local copies, waits for them, and re-layouts: 36.9 us -> 4.47 us
    psum x1 -> x0, blocking collectives: 21.6 us -> none  [device_program(): lax.psum(jnp.stack([jnp.stack(gain_a_acc), jnp.stack(gain_b_acc)]), 'tp')]
    reduce_sum x15 -> x1, other arithmetic: 21 us -> 1.3 us  [norm_rows(): jnp.mean(rows * rows, axis=-1, keepdims=True) + NORM_EPS]
  transfers between devices with their start and end apart: 32 -> 0, of which waited for: 27 -> 0; matrix products, arithmetic and copies ran while one was open for 28% -> 0% of each run, Pallas kernels for 0% -> 0%
where the time goes in v1:
time: 562 us; the launch traced here: 559 us
  Pallas kernels  528 us (94%)
  local copies, waits for them, and re-layouts  15.3 us (3%)
  other arithmetic  15.2 us (3%)
    pallas_call x1, Pallas kernels, run(): pl.pallas_call(self.body, out_shape=[self.out_shape((key[0],)) if key[0]...  528 us

profile of v1, /device:TPU:113, one launch (start us, length us, event | category | flops | bytes accessed | tf_op | source)
XLA Modules:
  0.0 559.2 jit_solution(4371902786282975274)
XLA Ops:
  0.6 0.0 copy-start
  0.7 0.0 copy-start.14
  0.7 1.3 fusion.3
  2.0 1.4 fusion.9
  3.4 0.0 copy-start.17
  3.4 0.0 copy-start.5
  3.4 2.1 fusion.5
  5.5 0.0 copy-done
  5.5 0.0 copy-done.14
  5.5 1.0 slice_bitcast_fusion.6
  6.5 0.0 copy-done.17
  6.5 0.0 copy-start.2
  6.5 0.0 copy-done.5
  6.5 1.0 fusion.7
  7.5 0.7 copy-done.2
  8.3 0.0 copy-start.1
  8.3 1.3 slice_bitcast_fusion
  9.6 0.9 copy-done.1
  10.4 0.7 fusion.6
  11.2 0.0 copy-start.3
  11.2 0.0 copy-start.4
  11.2 1.7 copy_bitcast_fusion
  12.9 0.0 copy-done.3
  12.9 0.9 copy-done.4
  13.8 1.7 slice_bitcast_fusion.1
  15.5 527.7 %shard_map.160 = (bf16[128,1024]{1,0:T(8,128)(2,1)}, bf16[128,1024]{1,0:T(8,128)(2,1)}, bf16[1024,384]{1,0:T(8,128)(2,1)}, bf16[1024,384]{1,0:T(8,128)(2,1)}, bf...) custom-call(bf16[128,1024]{1,0:T(8,128)(2,1)} %get-tuple-element.52., ...), custom_call_target="tpu_custom_call" | custom-call | tf_op jit(solution)/shard_map/pallas_call | solution.py:584
  543.3 0.0 copy-start.7
  543.3 2.0 pad_maximum_fusion.5
  545.2 1.4 fusion.8
  546.6 0.0 copy-start.6
  546.6 2.0 pad_maximum_fusion.6
  548.6 0.0 copy-done.7
  548.6 0.3 stack_reshape.12
  548.9 0.0 copy-done.6
  548.9 0.3 stack_reshape.13
  549.2 0.0 copy-start.15
  549.2 0.0 copy-start.16
  549.2 2.8 pad_maximum_fusion
  552.0 0.0 copy-done.15
  552.0 0.0 copy-done.16
  552.1 0.0 copy-start.12
  552.1 0.0 copy-start.13
  552.1 1.1 pad_maximum_fusion.4
  553.1 0.4 copy-done.12
  553.5 0.3 copy-done.13
  553.8 0.0 copy-start.10
  553.8 0.0 copy-start.11
  553.8 1.3 pad_maximum_fusion.1
  555.1 0.0 copy-done.10
  555.1 0.6 copy-done.11
  555.7 0.0 copy-start.8
  555.7 0.0 copy-start.9
  555.7 1.3 pad_maximum_fusion.2
  557.1 0.0 copy-done.8
  557.1 0.6 copy-done.9
  557.7 1.3 pad_maximum_fusion.3
  (1 shorter events, 0.0 us)
Async XLA Ops:
  0.6 4.8 copy-start
  0.7 4.8 copy-start.14
  3.4 3.1 copy-start.17
  3.4 3.1 copy-start.5
  6.5 1.8 copy-start.2
  8.3 2.2 copy-start.1
  11.2 1.8 copy-start.3
  11.2 2.6 copy-start.4
  543.3 5.3 copy-start.7
  546.6 2.2 copy-start.6
  549.2 2.9 copy-start.15
  549.2 2.9 copy-start.16
  552.1 1.4 copy-start.12
  552.1 1.7 copy-start.13
  553.8 1.3 copy-start.10
  553.8 1.9 copy-start.11
  555.7 1.3 copy-start.8
  555.7 1.9 copy-start.9

commit v2 on v1

--- a/solution.py
+++ b/solution.py
@@ -69,7 +69,7 @@
         if kind == GBUF:
             return (self.count, 2 * self.layers, w), F32
         if kind in (GA, GM):
-            return (1, w), F32
+            return (self.layers, w), F32
         if kind in (DK, DV):
             return (2 * c * r, HEAD), F32
         dims = {WQ: (w, self.qkv_w), WO: (self.mix_w, w), W1: (w, self.ff), W3: (w, self.ff), W2: (self.ff, w)}
@@ -113,10 +113,10 @@
         m, k = self.seq[n]
         ops = []
         kind, base, srow, gain, new, norm, slot, saved = self.comm_of(m, k)
-        reads = [sv[:3] for sv in saved]
-        writes = [(sv[3], m) for sv in saved]
+        reads = [sv[:3] for sv in saved] if k else [(XR, m, 0), (GA,)]
+        writes = [(sv[3], m) for sv in saved] + ([] if k else [(UR, m, 0)])
         if kind is not None:
-            reads += [(PREC, m), (RFU, m), (RFD, m), base] + [x for x in (srow, gain) if x]
+            reads += [(PREC, m), (RFU, m), (RFD, m), base] + [x for x in (srow, gain and gain[:1]) if x]
             if slot is not None:
                 reads.append((GP,))
                 writes.append((GP,))
@@ -202,10 +202,14 @@
 
     def body(self, *refs):
         pn = self.plan
-        ni, no, lo_ = len(self.live_in), len(self.live_out), len(self.results)
-        ins = dict(zip(self.live_in, refs[:ni]))
+        ni, no, lo_ = len(self.arrays), len(self.live_out), len(self.stacks)
+        ins = {}
+        for key in self.live_in:
+            q, idx = self.place[key]
+            ins[key] = refs[q] if idx is None else refs[q].at[idx]
         outs = dict(zip(self.live_out, refs[ni:ni + no]))
-        res = dict(zip(self.results, refs[ni + no:ni + no + lo_]))
+        piles = dict(zip(self.stacks, refs[ni + no:ni + no + lo_]))
+        res = {key: piles[key[:1]] if len(key) == 1 else piles[key[:1]].at[key[1]] for key in self.results}
         s = dict(zip(self.keys, refs[ni + no + lo_:-5]))
         lsem, ssem, rsem, psem, qsem = refs[-5:]
         rows, chips, count = pn.rows, pn.chips, pn.count
@@ -265,7 +269,17 @@
                 lo = h * h2
                 far[m].append((remote(red.at[cf, pl.ds(lo, h4)], s[(RFU, m)].at[pl.ds(h * h4, h4)], up, m, 4 * h, False),
                                remote(red.at[cf, pl.ds(lo + h4, h4)], s[(RFD, m)].at[pl.ds(h * h4, h4)], dn, m, 4 * h + 1, False)))
-                for d in far[m][h]:
+
+        def fold(m, c):
+            d = part_copy(m, c)
+            d.wait_recv()
+            s[(PREC, m)][c] = s[(PREC, m)][c] + s[(PART,)][c, pl.ds(pl.multiple_of(core * rows, 16), rows)]
+            d.wait_send()
+
+        def fold_far(m):
+            fold(m, cf)
+            for pair in far[m]:
+                for d in pair:
                     d.start()
 
         def rs_mid(m):
@@ -338,21 +352,24 @@
                 src_ref=s[(PART,)].at[t, pl.ds(pl.multiple_of(oc * rows, 16), rows)], dst_ref=s[(PREC, m)].at[t],
                 send_sem=psem.at[m, t], recv_sem=qsem.at[m, t], device_id={'tp': sib}, device_id_type=MESH)
 
-        def loop(fn, m=None, hook=None, at=0):
+        def loop(fn, m=None, hook=None, at=0, lo=0, hi=chips, spin=False):
+            def tile(t):
+                return lax.rem(chip + 2 + 3 * t, chips) if spin else t
+
             def step(t, carry):
-                fn(t)
+                fn(tile(t))
                 if m is not None:
                     @pl.when(t > 0)
                     def _():
-                        part_copy(m, t - 1).start()
+                        part_copy(m, tile(t - 1)).start()
                 if hook is not None:
                     @pl.when(t == at)
                     def _():
                         hook()
                 return carry
-            lax.fori_loop(0, chips, step, 0)
-            if m is not None:
-                part_copy(m, chips - 1).start()
+            lax.fori_loop(lo, hi, step, 0)
+            if m is not None and hi == chips:
+                part_copy(m, tile(chips - 1)).start()
 
 
         for n in range(self.first, self.last):
@@ -363,17 +380,22 @@
             for q, sv in enumerate(saved):
                 key = sv[:3]
                 need(key)
+                if k == 0:
+                    need((XR, m, 0), (GA,))
+                    s[key][...] = norm_rows(s[(XR, m, 0)][...].astype(F32), s[(GA,)][0:1]).astype(BF16)
                 full = s[(sv[3], m)]
                 full[chip, pl.ds(pl.multiple_of(core * rows, 16), rows)] = s[key][...]
-                st = ag_make(full, m, 0, rows, 12 + 8 * q)
-                for d in st:
-                    d.start()
-                gathers.append((full, m, 0, rows, 12 + 8 * q, st))
+                cut = [(0, rows, 12 + 8 * q)] if k else [(h * h2, h2, 28 + 8 * h) for h in halves]
+                for lo, size, first in cut:
+                    st = ag_make(full, m, lo, size, first)
+                    for d in st:
+                        d.start()
+                    gathers.append((full, m, lo, size, first, st))
             close()
 
             hook = None
             if kind is not None:
-                need(*[x for x in (base, srow, gain) if x])
+                need(*[x for x in (base, srow, gain and gain[:1]) if x])
                 if slot is not None:
                     need((GP,))
                 news = []
@@ -393,14 +415,15 @@
                 for x in ((BQ, BO) if comp == 3 else (B1, B3, B2) if comp == 2 else ()):
                     if (x, l + 1) in stores:
                         stores.pop((x, l + 1)).wait()
-                fn(s, need, loop, hook, pm, l, full)
-                red = s[(PREC, pm)]
-                for c in range(chips):
-                    d = part_copy(pm, c)
-                    d.wait_recv()
-                    red[c] = red[c] + s[(PART,)][c, pl.ds(pl.multiple_of(core * rows, 16), rows)]
-                    d.wait_send()
                 rs_far(pm)
+                early = functools.partial(fold_far, pm)
+                late = fn(s, need, loop, hook, pm, l, full, early, n == 1 or n == len(pn.seq) - 2)
+                if comp != 3 or l:
+                    early()
+                for c in (cu, cd, chip):
+                    fold(pm, c)
+                if late is not None:
+                    late()
                 if comp >= 2 and pm == pn.micro - 1:
                     for a, b in ((AQ, BQ), (AO, BO)) if comp == 3 else ((A1, B1), (A3, B3), (A2, B2)):
                         s[(b,)][...] = s[(a,)][...].astype(BF16)
@@ -456,12 +479,12 @@
                 x = s[srow][q].astype(F32)
                 scale = lax.rsqrt(jnp.mean(x * x, axis=-1, keepdims=True) + NORM_EPS)
                 s[(GP,)][slot:slot + 1] += jnp.sum(total * x * scale, axis=0, keepdims=True)
-                ct = total * s[gain][...]
+                ct = total * s[gain[:1]][gain[1]:gain[1] + 1]
                 total = scale * ct - x * (scale * scale * scale) * jnp.mean(ct * x, axis=-1, keepdims=True)
             val = (s[base][q].astype(F32) + total).astype(BF16)
             s[new][q] = val
             if kind == 0:
-                val = norm_rows(val.astype(F32), s[gain][...]).astype(BF16)
+                val = norm_rows(val.astype(F32), s[gain[:1]][gain[1]:gain[1] + 1]).astype(BF16)
                 s[norm][q] = val
             if kind == 1:
                 val = s[(GR, m)][q]
@@ -480,11 +503,11 @@
         qpos = lax.broadcasted_iota(jnp.int32, (total, rows2), 1) + t * rows2
         return jnp.where(kpos <= qpos, sc, -1e30)
 
-    def heads(self, qkv):
-        ow, total = self.plan.mix_w, 2 * self.plan.chips * self.plan.rows
-        return (qkv[:, :, ow:ow + HEAD].reshape(total, HEAD), qkv[:, :, ow + HEAD:ow + 2 * HEAD].reshape(total, HEAD))
-
-    def attn_f(self, s, need, loop, hook, m, l, full):
+    def heads(self, qkv, span):
+        ow, total = self.plan.mix_w, 2 * span * self.plan.rows
+        return (qkv[:span, :, ow:ow + HEAD].reshape(total, HEAD), qkv[:span, :, ow + HEAD:ow + 2 * HEAD].reshape(total, HEAD))
+
+    def attn_f(self, s, need, loop, hook, m, l, full, early, bare):
         need((WQ, l), (WO, l))
         qkv, mix, lse = s[(QKV, m, l)], s[(MIX, m, l)], s[(LSE, m, l)]
 
@@ -492,8 +515,8 @@
             qkv[t] = dot_nn(full[t], s[(WQ, l)][...]).astype(BF16)
         loop(proj)
 
-        def attend(t):
-            keys, vals = self.heads(qkv)
+        def attend(span, t):
+            keys, vals = self.heads(qkv, span)
             for h in range(self.plan.mix_w // HEAD):
                 cols = slice(h * HEAD, (h + 1) * HEAD)
                 sc = self.scores(t, keys, qkv[t, :, cols])
@@ -503,9 +526,11 @@
                 lse[t, h:h + 1] = top + jnp.log(tot)
                 mix[t, :, cols] = dot_tn((ex * (1.0 / tot)).astype(BF16), vals).astype(BF16)
             s[(PART,)][t] = dot_nn(mix[t], s[(WO, l)][...])
-        loop(attend, m, hook, 1)
-
-    def mlp_f(self, s, need, loop, hook, m, l, full):
+        size = 1 if bare else self.plan.chips // 2
+        for lo in range(0, self.plan.chips, size):
+            loop(functools.partial(attend, lo + size), m, hook if lo <= 1 < lo + size else None, 1, lo, lo + size)
+
+    def mlp_f(self, s, need, loop, hook, m, l, full, early, bare):
         need((W1, l), (W3, l), (W2, l))
 
         def tile(t):
@@ -524,7 +549,7 @@
             else:
                 s[key][...] = jnp.zeros_like(s[key])
 
-    def mlp_b(self, s, need, loop, hook, m, l, full):
+    def mlp_b(self, s, need, loop, hook, m, l, full, early, bare):
         need((W1, l), (W3, l), (W2, l))
         self.start_sums(s, need, m, ((A1,), (A3,), (A2,)))
         grad = s[(FN, m)]
@@ -544,7 +569,7 @@
             s[(PART,)][t] = dot_nt(dg, s[(W1, l)][...]) + dot_nt(dw, s[(W3, l)][...])
         loop(tile, m, hook, 2)
 
-    def attn_b(self, s, need, loop, hook, m, l, full):
+    def attn_b(self, s, need, loop, hook, m, l, full, early, bare):
         need((WQ, l), (WO, l), (QKV, m, l), (MIX, m, l), (LSE, m, l))
         self.start_sums(s, need, m, ((AQ,), (AO,)))
         grad, dqkv, dk, dv = s[(FN, m)], s[(DQKV,)], s[(DK,)], s[(DV,)]
@@ -552,47 +577,95 @@
         dk[...] = jnp.zeros_like(dk)
         dv[...] = jnp.zeros_like(dv)
 
-        def attend(t):
+        def attend(span, t):
+            size = 2 * span * self.plan.rows
             dh = grad[t]
-            s[(AO,)][...] += dot_tn(mix[t], dh)
+            if not bare:
+                s[(AO,)][...] += dot_tn(mix[t], dh)
             do = dot_nt(dh, s[(WO, l)][...]).astype(BF16)
-            keys, vals = self.heads(qkv)
+            keys, vals = self.heads(qkv, span)
             for h in range(self.plan.mix_w // HEAD):
                 cols = slice(h * HEAD, (h + 1) * HEAD)
                 q, doh = qkv[t, :, cols], do[:, cols]
                 prob = jnp.exp(self.scores(t, keys, q) - lse[t, h:h + 1])
-                dv[...] += dot_nn(prob.astype(BF16), doh)
+                dv[:size] += dot_nn(prob.astype(BF16), doh)
                 dp = dot_nt(vals, doh).astype(BF16).astype(F32)
                 rd = jnp.sum(dp * prob, axis=0, keepdims=True)
                 ds = (prob * (dp - rd) * HEAD ** -0.5).astype(BF16)
-                dk[...] += dot_nn(ds, q)
+                dk[:size] += dot_nn(ds, q)
                 dqkv[t, :, cols] = dot_tn(ds, keys).astype(BF16)
-        loop(attend, None, hook, 2)
+        step = 1 if bare else self.plan.chips // 2
+        for lo in range(0, self.plan.chips, step):
+            loop(functools.partial(attend, lo + step), None, hook if lo <= 2 < lo + step else None, 2, lo, lo + step)
         ow, shp = self.plan.mix_w, dqkv.shape[:2] + (HEAD,)
         dqkv[:, :, ow:ow + HEAD] = dk[...].astype(BF16).reshape(shp)
         dqkv[:, :, ow + HEAD:ow + 2 * HEAD] = dv[...].astype(BF16).reshape(shp)
 
         def tile(t):
+            if not bare:
+                s[(AQ,)][...] += dot_tn(full[t], dqkv[t])
+            s[(PART,)][t] = dot_nt(dqkv[t], s[(WQ, l)][...])
+        loop(tile, m, None if l else early, 2, spin=True)
+
+        def sums(t):
+            s[(AO,)][...] += dot_tn(mix[t], grad[t])
             s[(AQ,)][...] += dot_tn(full[t], dqkv[t])
-            s[(PART,)][t] = dot_nt(dqkv[t], s[(WQ, l)][...])
-        loop(tile, m)
+        return functools.partial(loop, sums) if bare else None
 
     def run(self, state):
         any_spec = pl.BlockSpec(memory_space=pl.ANY)
-        out_keys = self.live_out + self.results
         pn = self.plan
+        self.arrays, self.place = [], {}
+        for key in self.live_in:
+            arr, idx = state[key]
+            found = [q for q, other in enumerate(self.arrays) if other is arr]
+            if not found:
+                self.arrays.append(arr)
+            self.place[key] = (found[0] if found else len(self.arrays) - 1, idx)
+        self.stacks = []
+        for key in self.results:
+            if key[:1] not in self.stacks:
+                self.stacks.append(key[:1])
+        shapes = [self.out_shape(key) for key in self.live_out]
+        for kind in self.stacks:
+            shp, dtype = pn.shape(kind)
+            lead = () if kind == (GSUM,) else (pn.micro,) if kind[0] in (YR, GR) else (pn.layers,)
+            shapes.append(jax.ShapeDtypeStruct(lead + shp, dtype))
         vals = pl.pallas_call(
             self.body,
-            out_shape=[self.out_shape((key[0],)) if key[0] in (BQ, BO, B1, B3, B2) else self.out_shape(key) for key in out_keys],
-            in_specs=[any_spec] * len(self.live_in),
-            out_specs=[any_spec] * len(out_keys),
+            out_shape=shapes,
+            in_specs=[any_spec] * len(self.arrays),
+            out_specs=[any_spec] * len(shapes),
             scratch_shapes=[pltpu.VMEM(*pn.shape(key)) for key in self.keys] + [
-                pltpu.SemaphoreType.DMA((len(self.live_in) + len(out_keys),)),
+                pltpu.SemaphoreType.DMA((len(self.live_in) + len(self.live_out) + len(self.results),)),
                 pltpu.SemaphoreType.DMA((pn.micro, 52)), pltpu.SemaphoreType.DMA((pn.micro, 52)),
                 pltpu.SemaphoreType.DMA((pn.micro, pn.chips)), pltpu.SemaphoreType.DMA((pn.micro, pn.chips))],
             compiler_params=pltpu.CompilerParams(collective_id=self.cid, has_side_effects=True, vmem_limit_bytes=VMEM_BYTES),
-        )(*[state[key] for key in self.live_in])
-        state.update(zip(out_keys, vals))
+        )(*self.arrays)
+        state.update(zip(self.live_out + self.stacks, [(v, None) for v in vals]))
+
+
+def hand_over(arrays):
+    n = len(arrays)
+
+    def body(*refs):
+        src, dst, tmp, sem = refs[:n], refs[n:2 * n], refs[2 * n:3 * n], refs[3 * n]
+        first = [pltpu.make_async_copy(src[q], tmp[q], sem.at[0, q]) for q in range(n)]
+        second = [pltpu.make_async_copy(tmp[q], dst[q], sem.at[1, q]) for q in range(n)]
+        for d in first:
+            d.start()
+        for q in range(n):
+            first[q].wait()
+            second[q].start()
+        for d in second:
+            d.wait()
+
+    any_spec = pl.BlockSpec(memory_space=pl.ANY)
+    return pl.pallas_call(
+        body, out_shape=[jax.ShapeDtypeStruct(a.shape, a.dtype) for a in arrays],
+        in_specs=[any_spec] * n, out_specs=[any_spec] * n,
+        scratch_shapes=[pltpu.VMEM(a.shape, a.dtype) for a in arrays] + [pltpu.SemaphoreType.DMA((2, n))],
+        compiler_params=pltpu.CompilerParams(vmem_limit_bytes=VMEM_BYTES))(*arrays)
 
 
 def solution(mesh):
@@ -609,26 +682,18 @@
         wq = w_qkv.reshape(layers, width, -1)
         wo = w_out.reshape(layers, -1, width)
         plan = Plan(count, micro, layers, rows, width, wq.shape[2], wo.shape[1], w_gate.shape[2])
-        state = {}
+        state = {(GA,): (gain_attn, None), (GM,): (gain_mlp, None)}
         for m in range(micro):
-            state[(XR, m, 0)] = x_in[m]
-            state[(GR, m)] = y_cot[m]
-            state[(UR, m, 0)] = norm_rows(x_in[m].astype(F32), gain_attn[0:1]).astype(BF16)
+            state[(XR, m, 0)], state[(GR, m)] = (x_in, m), (y_cot, m)
         for l in range(layers):
             for key, arr in ((WQ, wq), (WO, wo), (W1, w_gate), (W3, w_up), (W2, w_down)):
-                state[(key, l)] = arr[l]
-            state[(GA, l)], state[(GM, l)] = gain_attn[l:l + 1], gain_mlp[l:l + 1]
+                state[(key, l)] = (arr, l)
         cuts = [0] + list(SPLITS) + [len(plan.seq)]
         for cid in range(len(cuts) - 1):
             Kernel(plan, cid, cuts[cid], cuts[cid + 1]).run(state)
-
-        def stack(key, shape):
-            return jnp.stack([state[(key, l)].reshape(shape) for l in range(layers)])
-
-        gsum = state[(GSUM,)]
-        return (jnp.stack([state[(YR, m)] for m in range(micro)]), jnp.stack([state[(GR, m)] for m in range(micro)]),
-                stack(BQ, w_qkv.shape[1:]), stack(BO, w_out.shape[1:]), stack(B1, w_gate.shape[1:]),
-                stack(B3, w_up.shape[1:]), stack(B2, w_down.shape[1:]), gsum[:layers], gsum[layers:])
+        y_out, grad_x, g_out, g_gate, g_up, g_down, gsum = hand_over([state[(x,)][0] for x in (YR, GR, BO, B1, B3, B2, GSUM)])
+        return (y_out, grad_x, state[(BQ,)][0].reshape(w_qkv.shape), g_out.reshape(w_out.shape), g_gate, g_up, g_down,
+                gsum[:layers], gsum[layers:])
 
     return jax.shard_map(device_program, mesh=mesh,
                          in_specs=(rows_p, rows_p, flat, flat, P(None, None, 'tp', None, None), head_p, cols_p, cols_p, down_p),

time: 562 us -> 539 us (0.959)
  other arithmetic: 15.2 us -> 0 us
  Pallas kernels: 528 us -> 520 us
  local copies, waits for them, and re-layouts: 15.3 us -> 9.46 us
    another operation x7 -> x0, other arithmetic: 11.7 us -> none  [the longest x5 7.82 us: stack(): return jnp.stack([state[key, l].reshape(shape) for l in range(layers)])]
    reshape x0 -> x2, local copies, waits for them, and re-layouts: none -> 8.06 us  [the longest x1 4.1 us: device_program(): wq = w_qkv.reshape(layers, width, -1)]
    pallas_call x1 -> x2, Pallas kernels: 528 us -> 520 us  [the longest x1 515 us: run(): pl.pallas_call(self.body, out_shape=shapes, in_specs=[any_spec] * len(sel...]
    squeeze x4 -> x0, local copies, waits for them, and re-layouts: 5.75 us -> none  [the longest x3 4.75 us: device_program(): state[key, l] = arr[l]]
where the time goes in v2:
time: 539 us; the launch traced here: 531 us
  Pallas kernels  520 us (96%)
  local copies, waits for them, and re-layouts  9.46 us (2%)
    pallas_call x1, Pallas kernels, run(): pl.pallas_call(self.body, out_shape=shapes, in_specs=[any_spec] * len(sel...  515 us

profile of v2, /device:TPU:113, one launch (start us, length us, event | category | flops | bytes accessed | tf_op | source)
XLA Modules:
  0.0 530.8 jit_solution(10302438687078161003)
XLA Ops:
  0.6 4.1 reshape.30.refs_2_
  4.7 514.6 %shard_map.160 = (bf16[2,128,1024]{2,1,0:T(8,128)(2,1)}, bf16[2,1024,384]{2,1,0:T(8,128)(2,1)}, bf16[2,1024,384]{2,1,0:T(8,128)(2,1)}, bf16[2,384,1024]{2,1,0:T(...) custom-call(bf16[2,128,1024]{2,1,0:T(8,128)(2,1)} %refs_0_.1, ...), custom_call_target="tpu_custom_call" | custom-call | tf_op jit(solution)/shard_map/pallas_call | solution.py:634
  519.4 5.6 %shard_map.161 = (bf16[2,128,1024]{2,1,0:T(8,128)(2,1)}, bf16[2,128,1024]{2,1,0:T(8,128)(2,1)}, bf16[2,256,1024]{2,1,0:T(8,128)(2,1)}, bf16[2,1024,384]{2,1,0:T(...) custom-call(bf16[2,128,1024]{2,1,0:T(8,128)(2,1)} %get-tuple-element.24.refs_0_, ...), custom_call_target="tpu_custom_call" | custom-call | tf_op jit(solution)/shard_map/pallas_call | solution.py:664
  525.0 1.4 fusion
  526.4 4.0 reshape.32
